TPU v7x, 512 devices: a whole 4x8x8 slice. The times are simulated.
512 devices in a mesh: seq: 64 (over y, x, core), head: 8 (over z).
Axes of the slice: x: 4, y: 8, z: 8, core: 2. Of those that a mesh axis runs over, the one named last changes fastest.
Arguments:
- queries: bfloat16 [8192, 8192], P('seq', 'head'), may hold values from -6 to 6
- keys: bfloat16 [8192, 8192], P('seq', 'head'), may hold values from -6 to 6
- values: bfloat16 [8192, 8192], P('seq', 'head'), may hold values from -48 to 48, as said below
- cotangent: bfloat16 [8192, 8192], P('seq', 'head'), may hold values from -6 to 6
- gain: float32 [8192], P('head'), may hold values from 0.1 to 1.9
Outputs:
- query_grad: bfloat16 [8192, 8192], P('seq', 'head')
- key_grad: bfloat16 [8192, 8192], P('seq', 'head')
- value_grad: bfloat16 [8192, 8192], P('seq', 'head')
Inputs may be any that keep to these rules, and one draw needn't show every extreme that they name: Real values.
All inputs are finite; a program needn't handle non-finite values.
Results may differ from a plain program's by a relative error of at most 0.0058.
Values sent between devices are 32-bit elements; how exact they have to be, the bound alone decides.
A program may use at most 128 MiB of HBM per device.

v0:
```python
import jax
import jax.numpy as jnp
from jax import lax
from jax.sharding import Mesh
from jax.sharding import PartitionSpec as P

HEAD_DIM = 128
SEQ = ("seq_0", "seq_1", "seq_2")


epsilon = 1e-05


def neutral_like(value, identity):
    return jnp.zeros_like(value) + jnp.asarray(identity, value.dtype)


def prefix_by_axis(value, axes, combine, identity, reverse):
    before = start = neutral_like(value, identity)
    so_far = value
    for axis in reversed(axes):
        count, mine = (lax.axis_size(axis), lax.axis_index(axis))
        pieces = lax.all_gather(so_far, axis)
        inside, so_far = (start, start)
        for k in reversed(range(count)) if reverse else range(count):
            passed = k > mine if reverse else k < mine
            so_far = combine(so_far, pieces[k])
            inside = jnp.where(passed, so_far, inside)
        before = combine(inside, before)
    return before


def sent_to_all(value, axis):
    count = lax.axis_size(axis)
    return lax.all_to_all(
        jnp.broadcast_to(value[None], (count, *value.shape)), axis, 0, 0, tiled=True
    )


def of_everyone(value, axis):
    return sent_to_all(value, axis).sum(axis=0)


def packed_total(arrays, axis):
    ravelled, at, done = (jnp.concatenate([a.reshape(-1) for a in arrays]), 0, [])
    so_far = of_everyone(ravelled, axis)
    for a in arrays:
        done.append(so_far[at : at + a.size].reshape(a.shape))
        at += a.size
    return tuple(done)


def causal(tokens):
    rows_index = lax.broadcasted_iota(jnp.int32, (tokens, tokens), 0)
    cols_index = lax.broadcasted_iota(jnp.int32, (tokens, tokens), 1)
    return (rows_index >= cols_index)[None, :, :]


def per_device(queries, keys, values, cotangent, gain):
    tokens, width_local = queries.shape
    heads_local = width_local // HEAD_DIM
    score_scale = HEAD_DIM ** (-0.5)
    total_width = width_local * lax.axis_size("head")
    causal_mask = causal(tokens)
    query_heads = queries.reshape(tokens, heads_local, HEAD_DIM)
    key_heads = keys.reshape(tokens, heads_local, HEAD_DIM)
    value_heads = values.reshape(tokens, heads_local, HEAD_DIM)
    local_state = jnp.einsum(
        "shd,she->hde", key_heads, value_heads, preferred_element_type=jnp.float32
    )
    prefix = prefix_by_axis(local_state, SEQ, jnp.add, jnp.zeros_like(local_state), False)
    prefix_low = prefix.astype(jnp.bfloat16)
    scores = (
        jnp.einsum("thd,shd->hts", query_heads, key_heads, preferred_element_type=jnp.float32)
        * score_scale
    )
    weights = jnp.where(causal_mask, scores, 0.0).astype(jnp.bfloat16)
    attended = jnp.einsum("hts,shd->thd", weights, value_heads, preferred_element_type=jnp.float32)
    attended = attended + score_scale * jnp.einsum(
        "thd,hde->the", query_heads, prefix_low, preferred_element_type=jnp.float32
    )
    attended = attended.reshape(tokens, width_local)
    scaled = cotangent.astype(jnp.float32) * gain[None, :]
    squares, cross_terms = packed_total(
        (jnp.sum(attended * attended, axis=1), jnp.sum(scaled * attended, axis=1)), "head"
    )
    inverse_rms = lax.rsqrt(squares / total_width + epsilon)
    normed = attended * inverse_rms[:, None]
    cross_mean = cross_terms * inverse_rms / total_width
    grad_attended = ((scaled - normed * cross_mean[:, None]) * inverse_rms[:, None]).astype(
        jnp.bfloat16
    )
    grad_heads = grad_attended.reshape(tokens, heads_local, HEAD_DIM)
    local_grad_state = jnp.einsum(
        "thd,the->hde", query_heads, grad_heads, preferred_element_type=jnp.float32
    )
    suffix = prefix_by_axis(local_grad_state, SEQ, jnp.add, jnp.zeros_like(local_grad_state), True)
    suffix_low = suffix.astype(jnp.bfloat16)
    grad_scores = (
        jnp.einsum("the,she->hts", grad_heads, value_heads, preferred_element_type=jnp.float32)
        * score_scale
    )
    grad_weights = jnp.where(causal_mask, grad_scores, 0.0).astype(jnp.bfloat16)
    query_grad = jnp.einsum(
        "hts,shd->thd", grad_weights, key_heads, preferred_element_type=jnp.float32
    )
    query_grad = query_grad + score_scale * jnp.einsum(
        "the,hde->thd", grad_heads, prefix_low, preferred_element_type=jnp.float32
    )
    key_grad = jnp.einsum(
        "hts,thd->shd", grad_weights, query_heads, preferred_element_type=jnp.float32
    )
    key_grad = key_grad + score_scale * jnp.einsum(
        "she,hde->shd", value_heads, suffix_low, preferred_element_type=jnp.float32
    )
    value_grad = jnp.einsum("hts,the->she", weights, grad_heads, preferred_element_type=jnp.float32)
    value_grad = value_grad + score_scale * jnp.einsum(
        "shd,hde->she", key_heads, suffix_low, preferred_element_type=jnp.float32
    )
    return (
        query_grad.reshape(tokens, width_local).astype(jnp.bfloat16),
        key_grad.reshape(tokens, width_local).astype(jnp.bfloat16),
        value_grad.reshape(tokens, width_local).astype(jnp.bfloat16),
    )


def solution(mesh):
    finer = Mesh(
        mesh.devices.reshape(8, 4, 2, mesh.shape["head"]), ("seq_0", "seq_1", "seq_2", "head")
    )
    in_specs = (P(SEQ, "head"), P(SEQ, "head"), P(SEQ, "head"), P(SEQ, "head"), P("head"))
    out_specs = (P(SEQ, "head"), P(SEQ, "head"), P(SEQ, "head"))
    return jax.shard_map(
        per_device, mesh=finer, in_specs=in_specs, out_specs=out_specs, check_vma=False
    )
```

profile of v0, /device:TPU:1, one launch (start us, length us, event | category | flops | bytes accessed | tf_op | source)
XLA Modules:
  0.0 277.5 jit_solution(10578391108742120236)
XLA Ops:
  7.2 1.0 copy.114
  8.3 0.2 copy.83
  8.5 1.0 fusion.25
  9.6 24.6 %all-gather.15.cloned.1.call-done = f32[16,128,128]{2,1,0:T(8,128)} async-done(((f32[8,128,128]{2,1,0:T(8,128)}), f32[16,128,128]{2,1,0:T(8,128)}) %all-gather.15.cloned.1.call-update) | async-done | bytes 1048592 | tf_op jit(solution)/shard_map/all_gather | solution.py:23
  34.2 2.1 slice_add_fusion.21
  36.4 35.9 %all-gather.19.cloned.1.call-done = f32[32,128,128]{2,1,0:T(8,128)} async-done(((f32[8,128,128]{2,1,0:T(8,128)}), f32[32,128,128]{2,1,0:T(8,128)}) %all-gather.19.cloned.1.call-update) | async-done | bytes 2097168 | tf_op jit(solution)/shard_map/all_gather | solution.py:23
  72.2 2.6 fusion.21
  75.0 2.0 fusion.9
  77.0 55.2 %all-gather.11.cloned.1.call-done = f32[8,8,128,128]{3,2,1,0:T(8,128)} async-done(((f32[1,8,128,128]{3,2,1,0:T(8,128)}), f32[8,8,128,128]{3,2,1,0:T(8,128)}) %all-gather.11.cloned.1.call-update) | async-done | bytes 4194320 | tf_op jit(solution)/shard_map/all_gather | solution.py:23
  132.2 3.0 %fusion.20 = bf16[1,8,128,128]{3,2,1,0:T(8,128)(2,1)S(1)} fusion(f32[8,8,128,128]{3,2,1,0:T(8,128)} %all-gather.11.cloned.1.call-done, f32[32,128,128]{2,1,0:T(8,128)S(1)} %copy-done.1, f32[16,128,128]{2,1,0:T(8,128)S(1)} %copy-done.3, pred[]{:T(512)S(6)} %gt.51, pred[]{:T(512)S(6)} %gt.52, pred[]{:T(512)S(6)} %gt.53, pred[]{:T(512)S(6)} %gt.54, ...), kind=kLoop, calls=%fused_computation.42 | loop fusion | flops 3670016 | bytes 7602190 | tf_op jit(solution)/shard_map/convert_element_type | solution.py:72
  135.2 0.3 fusion.7
  135.6 0.4 multiply_reduce_fusion.1
  136.4 13.5 %all_to_all.6 = f32[8,1,256]{2,1,0:T(1,128)S(1)} all-to-all(f32[8,1,256]{2,1,0:T(1,128)S(1)} %broadcast_in_dim.34), channel_id=1, replica_groups=mesh['seq_0'=8,'seq_1'=4,'seq_2'=2,'head'=8] {'head'}, dimensions={0} | all-to-all | bytes 16384 | tf_op jit(solution)/shard_map/all_to_all | solution.py:35
  150.3 0.2 convolution_bitcast_fusion.1
  150.5 1.0 copy.97
  151.6 13.8 %all-gather.17.cloned.1.call-done = f32[16,128,128]{2,1,0:T(8,128)} async-done(((f32[8,128,128]{2,1,0:T(8,128)}), f32[16,128,128]{2,1,0:T(8,128)}) %all-gather.17.cloned.1.call-update) | async-done | bytes 1048592 | tf_op jit(solution)/shard_map/all_gather | solution.py:23
  165.5 2.1 slice_add_fusion.10
  167.6 35.9 %all-gather.21.cloned.1.call-done = f32[32,128,128]{2,1,0:T(8,128)} async-done(((f32[8,128,128]{2,1,0:T(8,128)}), f32[32,128,128]{2,1,0:T(8,128)}) %all-gather.21.cloned.1.call-update) | async-done | bytes 2097168 | tf_op jit(solution)/shard_map/all_gather | solution.py:23
  203.5 2.4 fusion.17
  206.0 0.3 fusion.10
  206.4 1.4 fusion.5
  207.8 2.0 fusion.13
  209.8 1.8 copy.102
  211.6 2.1 fusion.47
  213.7 49.6 %all-gather.13.cloned.1.call-done = f32[8,8,128,128]{3,2,1,0:T(8,128)} async-done(((f32[1,8,128,128]{3,2,1,0:T(8,128)}), f32[8,8,128,128]{3,2,1,0:T(8,128)}) %all-gather.13.cloned.1.call-update) | async-done | bytes 4194320 | tf_op jit(solution)/shard_map/all_gather | solution.py:23
  263.3 3.0 %fusion.16 = bf16[1,8,128,128]{3,2,1,0:T(8,128)(2,1)S(1)} fusion(f32[8,8,128,128]{3,2,1,0:T(8,128)} %all-gather.13.cloned.1.call-done, f32[32,128,128]{2,1,0:T(8,128)S(1)} %copy-done.2, f32[16,128,128]{2,1,0:T(8,128)S(1)} %copy-done.4, pred[]{:T(512)S(6)} %lt.51, pred[]{:T(512)S(6)} %lt.52, pred[]{:T(512)S(6)} %lt.53, pred[]{:T(512)S(6)} %lt.54, ...), kind=kLoop, calls=%fused_computation.27 | loop fusion | flops 3670016 | bytes 7602190 | tf_op jit(solution)/shard_map/convert_element_type | solution.py:98
  266.3 0.7 copy-done.6
  267.0 0.3 fusion.4
  267.4 0.3 fusion.12
  267.7 0.9 copy.103
  268.5 1.3 fusion.11
  269.8 0.9 copy.104
  (58 shorter events, 1.3 us)
Async XLA Ops:
  7.2 1.3 copy-start
  7.2 27.0 %all-gather.15.cloned.1.call-start = ((), (), s32[]{:S(2)}) async-start(), calls=%async_computation.3 | async-start | bytes 1572864 | tf_op jit(solution)/shard_map/all_gather | solution.py:23
  8.5 27.9 %copy-start.7 = (bf16[128,8,128]{0,2,1:T(8,128)(2,1)}, bf16[128,8,128]{0,2,1:T(8,128)(2,1)S(1)}, u32[]{:S(2)}) copy-start(bf16[128,8,128]{0,2,1:T(8,128)(2,1)S(1)} %copy.83) | copy-start | bytes 786436
  9.6 62.7 %all-gather.19.cloned.1.call-start = ((), (), s32[]{:S(2)}) async-start(), calls=%async_computation.5 | async-start | bytes 2621440 | tf_op jit(solution)/shard_map/all_gather | solution.py:23
  36.3 95.9 %copy-start.3 = (f32[16,128,128]{2,1,0:T(8,128)S(1)}, f32[16,128,128]{2,1,0:T(8,128)}, u32[]{:S(2)}) copy-start(f32[16,128,128]{2,1,0:T(8,128)} %all-gather.15.cloned.1.call-done) | copy-start | bytes 3145732
  36.3 95.8 %all-gather.11.cloned.1.call-start = ((), (), s32[]{:S(2)}) async-start(), calls=%async_computation.1 | async-start | bytes 4718592 | tf_op jit(solution)/shard_map/all_gather | solution.py:23
  72.2 59.9 %copy-start.1 = (f32[32,128,128]{2,1,0:T(8,128)S(1)}, f32[32,128,128]{2,1,0:T(8,128)}, u32[]{:S(2)}) copy-start(f32[32,128,128]{2,1,0:T(8,128)} %all-gather.19.cloned.1.call-done) | copy-start | bytes 6291460
  74.9 90.6 %all-gather.17.cloned.1.call-start = ((), (), s32[]{:S(2)}) async-start(), calls=%async_computation.4 | async-start | bytes 1572864 | tf_op jit(solution)/shard_map/all_gather | solution.py:23
  132.2 3.0 %copy-start.8 = (bf16[128,1024]{1,0:T(8,128)(2,1)S(1)}, bf16[128,1024]{1,0:T(8,128)(2,1)}, u32[]{:S(2)}) copy-start(bf16[128,1024]{1,0:T(8,128)(2,1)} %param.5) | copy-start | bytes 786436
  132.2 3.4 %copy-start.17 = (bf16[8,128,128]{2,1,0:T(8,128)(2,1)S(1)}, bf16[8,128,128]{2,1,0:T(8,128)(2,1)}, u32[]{:S(2)}) copy-start(bf16[8,128,128]{2,1,0:T(8,128)(2,1)} %fusion.9) | copy-start | bytes 786436
  135.2 0.7 copy-start.11
  135.2 1.0 copy-start.16
  135.2 1.0 copy-start.18
  135.9 14.4 %copy-start.9 = (bf16[128,1024]{1,0:T(8,128)(2,1)S(1)}, bf16[128,1024]{1,0:T(8,128)(2,1)}, u32[]{:S(2)}) copy-start(bf16[128,1024]{1,0:T(8,128)(2,1)} %param.5) | copy-start | bytes 786436
  150.3 55.7 %copy-start.5 = (bf16[128,1024]{0,1:T(8,128)(2,1)}, bf16[128,1024]{0,1:T(8,128)(2,1)S(1)}, u32[]{:S(2)}) copy-start(bf16[128,1024]{0,1:T(8,128)(2,1)S(1)} %copy.110) | copy-start | bytes 786436
  151.6 51.9 %all-gather.21.cloned.1.call-start = ((), (), s32[]{:S(2)}) async-start(), calls=%async_computation.6 | async-start | bytes 2621440 | tf_op jit(solution)/shard_map/all_gather | solution.py:23
  167.6 95.7 %all-gather.13.cloned.1.call-start = ((), (), s32[]{:S(2)}) async-start(), calls=%async_computation.2 | async-start | bytes 4718592 | tf_op jit(solution)/shard_map/all_gather | solution.py:23
  206.4 3.4 %copy-start.13 = (bf16[8,128,128]{2,1,0:T(8,128)(2,1)}, bf16[8,128,128]{2,1,0:T(8,128)(2,1)S(1)}, u32[]{:S(2)}) copy-start(bf16[8,128,128]{2,1,0:T(8,128)(2,1)S(1)} %fusion.10) | copy-start | bytes 786436
  206.4 56.9 %copy-start.2 = (f32[32,128,128]{2,1,0:T(8,128)S(1)}, f32[32,128,128]{2,1,0:T(8,128)}, u32[]{:S(2)}) copy-start(f32[32,128,128]{2,1,0:T(8,128)} %all-gather.21.cloned.1.call-done) | copy-start | bytes 6291460
  206.4 56.9 %copy-start.4 = (f32[16,128,128]{2,1,0:T(8,128)S(1)}, f32[16,128,128]{2,1,0:T(8,128)}, u32[]{:S(2)}) copy-start(f32[16,128,128]{2,1,0:T(8,128)} %all-gather.17.cloned.1.call-done) | copy-start | bytes 3145732
  263.3 4.0 %copy-start.10 = (bf16[128,1024]{1,0:T(8,128)(2,1)S(1)}, bf16[128,1024]{1,0:T(8,128)(2,1)}, u32[]{:S(2)}) copy-start(bf16[128,1024]{1,0:T(8,128)(2,1)} %param.5) | copy-start | bytes 786436
  263.3 4.1 %copy-start.14 = (bf16[8,128,128]{2,1,0:T(8,128)(2,1)S(1)}, bf16[8,128,128]{2,1,0:T(8,128)(2,1)}, u32[]{:S(2)}) copy-start(bf16[8,128,128]{2,1,0:T(8,128)(2,1)} %copy-done.13) | copy-start | bytes 786436
  266.3 0.7 copy-start.6
  267.0 1.5 copy-start.12
  267.0 1.5 copy-start.15
Sparse Core Ops, SparseCore 0:
  10.1 24.0 all-gather.14
  36.4 35.7 all-gather.18
  75.0 57.1 all-gather.10
  151.7 13.7 all-gather.16
  167.7 35.7 all-gather.20
  206.1 57.1 all-gather.12
where the time goes:
time: 278 us; the launch traced here: 277 us
  waiting for transfers between devices  215 us (77%)
  other arithmetic  15.6 us (6%)
  between operations  14.4 us (5%)
  blocking collectives  13.5 us (5%)
  matrix products  11.7 us (4%)
  local copies, waits for them, and re-layouts  7.04 us (3%)
    all_gather x6, waiting for transfers between devices, prefix_by_axis(): pieces = lax.all_gather(so_far, axis)  215 us
    all_to_all x1, blocking collectives, sent_to_all(): lax.all_to_all(jnp.broadcast_to(value[None], (count, *value.shape)), axis...  13.5 us
    add x4, other arithmetic, prefix_by_axis(): so_far = combine(so_far, pieces[k])  9.17 us
  transfers between devices with their start and end apart: 6, of which 6 were waited for; matrix products, arithmetic and copies ran while one was open for 3% of the time, Pallas kernels for 0%

commit v1 on v0

v1 whole, which is shorter than its diff:
```python
import functools

import jax
import jax.numpy as jnp
from jax import lax
from jax.experimental import pallas as pl
from jax.experimental.pallas import tpu as pltpu
from jax.sharding import PartitionSpec as P

HEAD_DIM = 128
EPSILON = 1e-05
ROWS, COLUMNS = 8, 4
CHIPS = ROWS * COLUMNS
PEERS = CHIPS - 1
MESH = pl.DeviceIdType.MESH
F32, BF16 = jnp.float32, jnp.bfloat16


def dot(a, b, over):
    return lax.dot_general(a, b, ((over[:1], over[1:]), ((), ())), preferred_element_type=F32)


def ring_offset(k, size):
    return size // 2 + (1 - 2 * lax.rem(k, 2)) * lax.div(k + 1, 2)


def kernel(
    stacks, mine,
    q_hbm, k_hbm, v_hbm, cot_hbm, gain_ref,
    dq_hbm, dk_hbm, dv_hbm,
    tok, part, cot_own, cot_part, stage, came, scaled,
    blocks, state_out, state, gathered, scanned, prefix, low,
    weights, attended, stats, grads, late, suffix_low,
    grad_f32, grad_came, out_low,
    load_sem, store_sem, core_send, core_recv, go_send, go_recv, back_send, back_recv, stat_send, stat_recv,
):
    seq, z = lax.axis_index("seq"), lax.axis_index("head")
    core = lax.rem(seq, 2)
    other = 1 - core
    chip = lax.div(seq, 2)
    x, y = lax.rem(chip, COLUMNS), lax.div(chip, COLUMNS)
    heads = mine // HEAD_DIM
    scale = HEAD_DIM ** (-0.5)
    width = 2 * mine * stacks
    tokens = tok.shape[2]
    piece = state.shape[2]

    own_cols = pl.ds(pl.multiple_of(core * mine, mine), mine)
    part_cols = pl.ds(pl.multiple_of(other * mine, mine), mine)

    def col(j):
        return pl.ds(j * HEAD_DIM, HEAD_DIM)

    arrays = (q_hbm, k_hbm, v_hbm, cot_hbm)

    def load(a, own):
        if a == 3:
            target = cot_own if own else cot_part
        else:
            target = tok.at[a, core] if own else part.at[a]
        return pltpu.make_async_copy(
            arrays[a].at[:, own_cols if own else part_cols], target, load_sem.at[2 * a + int(own)]
        )

    for a in (1, 2):
        load(a, False).start()
    for a in (1, 2):
        load(a, True).start()
    for a in (0, 3):
        load(a, False).start()
        load(a, True).start()

    def chip_at(i):
        down = lax.rem(y + ring_offset(lax.div(i, COLUMNS), ROWS), ROWS)
        right = lax.rem(x + ring_offset(lax.rem(i, COLUMNS), COLUMNS), COLUMNS)
        return down * COLUMNS + right

    def stack_at(i):
        return {
            "seq": 2 * chip + lax.rem(core + lax.rem(i + 1, 2), 2),
            "head": lax.rem(z + lax.div(i + 1, 2), stacks),
        }

    stack_peers = 2 * stacks - 1

    def each(count, action):
        lax.fori_loop(0, count, lambda i, none: (action(i), none)[1], 0)

    barrier = pltpu.get_barrier_semaphore()

    def greet(target):
        pl.semaphore_signal(barrier, inc=1, device_id=target, device_id_type=MESH)

    each(PEERS, lambda i: greet({"seq": 2 * chip_at(i) + core, "head": z}))
    each(stack_peers, lambda i: greet(stack_at(i)))

    def to_core(src, dst, at):
        return pltpu.make_async_remote_copy(
            src_ref=src, dst_ref=dst, send_sem=core_send.at[at], recv_sem=core_recv.at[at],
            device_id={"seq": 2 * chip + other, "head": z}, device_id_type=MESH,
        )

    def go(s, i):
        target = chip_at(i)
        return pltpu.make_async_remote_copy(
            src_ref=state.at[s, target], dst_ref=gathered.at[s, chip],
            send_sem=go_send.at[s, i], recv_sem=go_recv.at[s, i],
            device_id={"seq": 2 * target + core, "head": z}, device_id_type=MESH,
        )

    def back(s, i):
        target = chip_at(i)
        return pltpu.make_async_remote_copy(
            src_ref=scanned.at[s, target], dst_ref=prefix.at[s, chip],
            send_sem=back_send.at[s, i], recv_sem=back_recv.at[s, i],
            device_id={"seq": 2 * target + core, "head": z}, device_id_type=MESH,
        )

    def scan_out(s):
        each(PEERS, lambda i: go(s, i).start())
        gathered[s, chip] = state[s, chip]

    def scan_back(s, reverse):
        each(PEERS, lambda i: go(s, i).wait_recv())
        so_far = jnp.zeros((piece, HEAD_DIM), F32)
        for p in reversed(range(CHIPS)) if reverse else range(CHIPS):
            scanned[s, p] = so_far
            so_far = so_far + gathered[s, p]
        each(PEERS, lambda i: back(s, i).start())
        prefix[s, chip] = scanned[s, chip]

    def head_of(ref, s, j):
        per_head = HEAD_DIM // piece
        return ref[s, pl.ds(j * per_head, per_head)].reshape(HEAD_DIM, HEAD_DIM)

    def put_state(s, j, value):
        per_head = HEAD_DIM // piece
        state[s, pl.ds(j * per_head, per_head)] = value.reshape(per_head, piece, HEAD_DIM)

    for a in (1, 2):
        load(a, False).wait()
    for j in range(heads):
        state_out[j] = dot(part[1, :, col(j)], part[2, :, col(j)], (0, 0))
    pl.semaphore_wait(barrier, PEERS + stack_peers)
    to_core(state_out, blocks.at[core], 0).start()
    for a in (1, 2):
        load(a, True).wait()
    for j in range(heads):
        blocks[core, j] = dot(tok[1, core, :, col(j)], tok[2, core, :, col(j)], (0, 0))
    to_core(state_out, blocks.at[other], 0).wait_recv()
    for j in range(heads):
        put_state(0, j, blocks[0, j] + blocks[1, j])
    scan_out(0)

    for n, a in enumerate((1, 2, 0)):
        if a == 0:
            load(0, False).wait()
        stage[n] = part[a].astype(F32)
        to_core(stage.at[n], came.at[n], 1 + n).start()
    load(3, False).wait()
    stage[3] = cot_part[...].astype(F32)
    to_core(stage.at[3], came.at[3], 4).start()

    causal = lax.broadcasted_iota(jnp.int32, (tokens, tokens), 0) >= lax.broadcasted_iota(
        jnp.int32, (tokens, tokens), 1
    )

    def masked(product):
        return jnp.where(causal, product * scale, 0.0).astype(BF16)

    def gain_of(j):
        return gain_ref[pl.ds(core * heads + j, 1), :]

    def within_block(b):
        for j in range(heads):
            w = masked(dot(tok[0, b, :, col(j)], tok[1, b, :, col(j)], (1, 1)))
            weights[b, :, col(j)] = w
            attended[b, :, col(j)] = dot(w, tok[2, b, :, col(j)], (1, 0))

    load(0, True).wait()
    load(3, True).wait()
    for j in range(heads):
        scaled[core, :, col(j)] = cot_own[:, col(j)].astype(F32) * gain_of(j)
    within_block(core)

    scan_back(0, False)
    for n, a in enumerate((1, 2, 0)):
        to_core(stage.at[n], came.at[n], 1 + n).wait_recv()
        tok[a, other] = came[n].astype(BF16)
    to_core(stage.at[3], came.at[3], 4).wait_recv()
    for j in range(heads):
        scaled[other, :, col(j)] = came[3, :, col(j)] * gain_of(j)
    within_block(other)

    each(PEERS, lambda i: back(0, i).wait_recv())
    squares = [jnp.zeros((tokens, HEAD_DIM), F32) for _ in range(2)]
    crosses = [jnp.zeros((tokens, HEAD_DIM), F32) for _ in range(2)]
    for j in range(heads):
        before = head_of(prefix, 0, j)
        low[0, j] = before.astype(BF16)
        low[1, j] = (before + blocks[0, j]).astype(BF16)
        for b in range(2):
            att = attended[b, :, col(j)] + scale * dot(tok[0, b, :, col(j)], low[b, j], (1, 0))
            attended[b, :, col(j)] = att
            squares[b] = squares[b] + att * att
            crosses[b] = crosses[b] + att * scaled[b, :, col(j)]
    me = 2 * z + core
    for r, sums in enumerate(squares + crosses):
        stats[me, pl.ds(r, 1), :] = jnp.sum(sums.T, axis=0, keepdims=True)

    def share(i):
        return pltpu.make_async_remote_copy(
            src_ref=stats.at[me], dst_ref=stats.at[me], send_sem=stat_send.at[i], recv_sem=stat_recv.at[i],
            device_id=stack_at(i), device_id_type=MESH,
        )

    def share_in(i):
        return pltpu.make_async_remote_copy(
            src_ref=stats.at[me], dst_ref=stats.at[me], send_sem=stat_send.at[i], recv_sem=stat_recv.at[i],
            device_id=stack_at(i), device_id_type=MESH,
        )

    each(stack_peers, lambda i: share(i).start())
    each(stack_peers, lambda i: share_in(i).wait_recv())
    total = stats[0]
    for p in range(1, 2 * stacks):
        total = total + stats[p]
    inverse_rms = lax.rsqrt(total[0:2] / width + EPSILON)
    cross_mean = total[2:4] * inverse_rms / width

    def down(row):
        return jnp.broadcast_to(row, (HEAD_DIM, tokens)).T

    inverse = [down(inverse_rms[b : b + 1]) for b in range(2)]
    cross = [down(cross_mean[b : b + 1]) for b in range(2)]
    for j in range(heads):
        sums = []
        for b in range(2):
            normed = attended[b, :, col(j)] * inverse[b]
            grad = ((scaled[b, :, col(j)] - normed * cross[b]) * inverse[b]).astype(BF16)
            grads[b, :, col(j)] = grad
            sums.append(dot(tok[0, b, :, col(j)], grad, (0, 0)))
        late[j] = sums[1]
        put_state(1, j, sums[0] + sums[1])
    scan_out(1)

    def without_suffix(b):
        for j in range(heads):
            grad = grads[b, :, col(j)]
            gw = masked(dot(grad, tok[2, b, :, col(j)], (1, 1)))
            grad_f32[0, b, :, col(j)] = dot(gw, tok[1, b, :, col(j)], (1, 0)) + scale * dot(
                grad, low[b, j], (1, 1)
            )
            grad_f32[1, b, :, col(j)] = dot(gw, tok[0, b, :, col(j)], (0, 0))
            grad_f32[2, b, :, col(j)] = dot(weights[b, :, col(j)], grad, (0, 0))

    outputs = (dq_hbm, dk_hbm, dv_hbm)

    def give(n):
        return to_core(grad_f32.at[n, other], grad_came.at[n], 5 + n)

    def store(n, own):
        return pltpu.make_async_copy(
            out_low.at[n, 0 if own else 1], outputs[n].at[:, own_cols if own else part_cols],
            store_sem.at[2 * n + int(own)],
        )

    without_suffix(other)
    give(0).start()
    without_suffix(core)
    out_low[0, 0] = grad_f32[0, core].astype(BF16)
    store(0, True).start()

    scan_back(1, True)
    give(0).wait_recv()
    out_low[0, 1] = grad_came[0].astype(BF16)
    store(0, False).start()

    each(PEERS, lambda i: back(1, i).wait_recv())
    for j in range(heads):
        after = head_of(prefix, 1, j)
        suffix_low[0, j] = (after + late[j]).astype(BF16)
        suffix_low[1, j] = after.astype(BF16)

    def with_suffix(b):
        for j in range(heads):
            suffix = suffix_low[b, j]
            grad_f32[1, b, :, col(j)] += scale * dot(tok[2, b, :, col(j)], suffix, (1, 1))
            grad_f32[2, b, :, col(j)] += scale * dot(tok[1, b, :, col(j)], suffix, (1, 0))

    with_suffix(other)
    for n in (1, 2):
        give(n).start()
    with_suffix(core)
    for n in (1, 2):
        out_low[n, 0] = grad_f32[n, core].astype(BF16)
        store(n, True).start()
    for n in (1, 2):
        give(n).wait_recv()
        out_low[n, 1] = grad_came[n].astype(BF16)
        store(n, False).start()

    to_core(state_out, blocks.at[core], 0).wait_send()
    for n in range(4):
        to_core(stage.at[n], came.at[n], 1 + n).wait_send()
    for s in range(2):
        each(PEERS, lambda i: go(s, i).wait_send())
        each(PEERS, lambda i: back(s, i).wait_send())
    each(stack_peers, lambda i: share(i).wait_send())
    for n in range(3):
        give(n).wait_send()
        store(n, True).wait()
        store(n, False).wait()


def per_device(stacks, queries, keys, values, cotangent, gain):
    tokens, local = queries.shape
    mine = local // 2
    heads = mine // HEAD_DIM
    piece = heads * HEAD_DIM // CHIPS
    anywhere = pl.BlockSpec(memory_space=pl.ANY)
    out = jax.ShapeDtypeStruct((tokens, local), BF16)
    dma = pltpu.SemaphoreType.DMA
    return pl.pallas_call(
        functools.partial(kernel, stacks, mine),
        out_shape=(out, out, out),
        in_specs=[anywhere] * 4 + [pl.BlockSpec(memory_space=pltpu.VMEM)],
        out_specs=(anywhere,) * 3,
        scratch_shapes=[
            pltpu.VMEM((3, 2, tokens, mine), BF16),
            pltpu.VMEM((3, tokens, mine), BF16),
            pltpu.VMEM((tokens, mine), BF16),
            pltpu.VMEM((tokens, mine), BF16),
            pltpu.VMEM((4, tokens, mine), F32),
            pltpu.VMEM((4, tokens, mine), F32),
            pltpu.VMEM((2, tokens, mine), F32),
            pltpu.VMEM((2, heads, HEAD_DIM, HEAD_DIM), F32),
            pltpu.VMEM((heads, HEAD_DIM, HEAD_DIM), F32),
            pltpu.VMEM((2, CHIPS, piece, HEAD_DIM), F32),
            pltpu.VMEM((2, CHIPS, piece, HEAD_DIM), F32),
            pltpu.VMEM((2, CHIPS, piece, HEAD_DIM), F32),
            pltpu.VMEM((2, CHIPS, piece, HEAD_DIM), F32),
            pltpu.VMEM((2, heads, HEAD_DIM, HEAD_DIM), BF16),
            pltpu.VMEM((2, tokens, mine), BF16),
            pltpu.VMEM((2, tokens, mine), F32),
            pltpu.VMEM((2 * stacks, 4, tokens), F32),
            pltpu.VMEM((2, tokens, mine), BF16),
            pltpu.VMEM((heads, HEAD_DIM, HEAD_DIM), F32),
            pltpu.VMEM((2, heads, HEAD_DIM, HEAD_DIM), BF16),
            pltpu.VMEM((3, 2, tokens, mine), F32),
            pltpu.VMEM((3, tokens, mine), F32),
            pltpu.VMEM((3, 2, tokens, mine), BF16),
            dma((8,)), dma((6,)),
            dma((8,)), dma((8,)),
            dma((2, PEERS)), dma((2, PEERS)), dma((2, PEERS)), dma((2, PEERS)),
            dma((2 * stacks - 1,)), dma((2 * stacks - 1,)),
        ],
        compiler_params=pltpu.CompilerParams(collective_id=0, has_side_effects=True),
        name="attention",
    )(queries, keys, values, cotangent, gain.reshape(2 * heads, HEAD_DIM))


def solution(mesh):
    spec = P("seq", "head")
    return jax.shard_map(
        functools.partial(per_device, mesh.shape["head"]),
        mesh=mesh,
        in_specs=(spec, spec, spec, spec, P("head")),
        out_specs=(spec, spec, spec),
        check_vma=False,
    )
```

time: 278 us -> 70.2 us (0.25)
  waiting for transfers between devices: 215 us -> 0 us
  Pallas kernels: 0 us -> 65.9 us
  other arithmetic: 15.6 us -> 0 us
  between operations: 14.4 us -> 0.65 us
  blocking collectives: 13.5 us -> 0 us
  matrix products: 11.7 us -> 0 us
  local copies, waits for them, and re-layouts: 7.04 us -> 3.46 us
    all_gather x6 -> x0, waiting for transfers between devices: 215 us -> none  [prefix_by_axis(): pieces = lax.all_gather(so_far, axis)]
    pallas_call x0 -> x1, Pallas kernels: none -> 65.9 us  [per_device(): pl.pallas_call(functools.partial(kernel, stacks, mine), out_shape=(out, o...]
    all_to_all x1 -> x0, blocking collectives: 13.5 us -> none  [sent_to_all(): lax.all_to_all(jnp.broadcast_to(value[None], (count, *value.shape)), axis...]
    dot_general x12 -> x0, matrix products: 11.7 us -> none  [the longest x1 2.1 us: per_device(): jnp.einsum('hts,the->she', weights, grad_heads, preferred_element_type=jn...]
    add x4 -> x0, other arithmetic: 9.17 us -> none  [prefix_by_axis(): so_far = combine(so_far, pieces[k])]
    convert_element_type x3 -> x0, other arithmetic: 6.21 us -> none  [the longest x1 3.02 us: per_device(): prefix_low = prefix.astype(jnp.bfloat16)]
  transfers between devices with their start and end apart: 6 -> 0, of which waited for: 6 -> 0; matrix products, arithmetic and copies ran while one was open for 3% -> 0% of each run, Pallas kernels for 0% -> 0%
where the time goes in v1:
time: 70.2 us; the launch traced here: 70 us
  Pallas kernels  65.9 us (94%)
  local copies, waits for them, and re-layouts  3.46 us (5%)
    pallas_call x1, Pallas kernels, per_device(): pl.pallas_call(functools.partial(kernel, stacks, mine), out_shape=(out, o...  65.9 us
    unnamed x7, local copies, waits for them, and re-layouts  3.46 us

profile of v1, /device:TPU:1, one launch (start us, length us, event | category | flops | bytes accessed | tf_op | source)
XLA Modules:
  0.0 70.0 jit_solution(9170319226204668813)
XLA Ops:
  0.6 65.9 %attention.1 = (bf16[128,1024]{1,0:T(8,128)(2,1)}, bf16[128,1024]{1,0:T(8,128)(2,1)}, bf16[128,1024]{1,0:T(8,128)(2,1)}) custom-call(bf16[128,1024]{1,0:T(8,128)(2,1)} %q_hbm.1, bf16[128,1024]{1,0:T(8,128)(2,1)} %k_hbm.1, bf16[128,1024]{1,0:T(8,128)(2,1)} %v_hbm.1, bf16[128,1024]{1,0:T(8,128)(2,1)} %cot_hbm.1, f32[8,128]{1,0:T(8,128)} %bitcast.1), custom_call_target="tpu_custom_call" | custom-call | tf_op jit(solution)/shard_map/attention/pallas_call | solution.py:324
  66.5 0.0 copy-start.1
  66.5 1.7 %copy.11 = bf16[128,1024]{1,0:T(8,128)(2,1)} copy(bf16[128,1024]{1,0:T(8,128)(2,1)} %get-tuple-element.6) | data formatting | bytes 524288
  68.2 0.0 copy-done.1
  68.2 0.0 copy-start
  68.2 0.7 %copy.12 = bf16[128,1024]{1,0:T(8,128)(2,1)} copy(bf16[128,1024]{1,0:T(8,128)(2,1)S(1)} %copy-done.1) | data formatting | bytes 524288
  68.9 0.3 copy-done
  69.3 0.7 %copy.13 = bf16[128,1024]{1,0:T(8,128)(2,1)} copy(bf16[128,1024]{1,0:T(8,128)(2,1)S(1)} %copy-done) | data formatting | bytes 524288
Async XLA Ops:
  66.5 1.7 %copy-start.1 = (bf16[128,1024]{1,0:T(8,128)(2,1)S(1)}, bf16[128,1024]{1,0:T(8,128)(2,1)}, u32[]{:S(2)}) copy-start(bf16[128,1024]{1,0:T(8,128)(2,1)} %get-tuple-element.7) | copy-start | bytes 786436
  68.2 1.0 %copy-start = (bf16[128,1024]{1,0:T(8,128)(2,1)S(1)}, bf16[128,1024]{1,0:T(8,128)(2,1)}, u32[]{:S(2)}) copy-start(bf16[128,1024]{1,0:T(8,128)(2,1)} %get-tuple-element.8) | copy-start | bytes 786436

commit v2 on v1

v2 whole, which is shorter than its diff:
```python
import functools

import jax
import jax.numpy as jnp
from jax import lax
from jax.experimental import pallas as pl
from jax.experimental.pallas import tpu as pltpu
from jax.sharding import PartitionSpec as P

HEAD_DIM = 128
EPSILON = 1e-05
ROWS, COLUMNS = 8, 4
CHIPS = ROWS * COLUMNS
PEERS = CHIPS - 1
CHUNKS = 2
MESH = pl.DeviceIdType.MESH
F32, BF16 = jnp.float32, jnp.bfloat16


def dot(a, b, over):
    return lax.dot_general(a, b, ((over[:1], over[1:]), ((), ())), preferred_element_type=F32)


def ring_offsets(size):
    return sorted(range(size), key=lambda d: -min(d, size - d))


def kernel(
    stacks, mine,
    q_hbm, k_hbm, v_hbm, cot_hbm, gain_hbm,
    result,
    gain, tok, part, cot_own, cot_part, stage, came, scaled,
    blocks, state_out, state, gathered, scanned, prefix, low,
    weights, attended, stats, grads, late,
    grad_f32, grad_came,
    load_sem, core_send, core_recv, go_send, go_recv, back_send, back_recv, stat_send, stat_recv,
):
    seq, z = lax.axis_index("seq"), lax.axis_index("head")
    core = lax.rem(seq, 2)
    other = 1 - core
    chip = lax.div(seq, 2)
    x, y = lax.rem(chip, COLUMNS), lax.div(chip, COLUMNS)
    heads = mine // HEAD_DIM
    per_chunk = heads // CHUNKS
    scale = HEAD_DIM ** (-0.5)
    width = 2 * mine * stacks
    tokens = tok.shape[2]
    piece = state.shape[3]
    per_head = HEAD_DIM // piece

    own_cols = pl.ds(pl.multiple_of(core * mine, mine), mine)
    part_cols = pl.ds(pl.multiple_of(other * mine, mine), mine)

    def col(j):
        return pl.ds(j * HEAD_DIM, HEAD_DIM)

    def heads_of(chunk):
        return range(chunk * per_chunk, (chunk + 1) * per_chunk)

    arrays = (q_hbm, k_hbm, v_hbm, cot_hbm)

    def load(a, own):
        if a == 3:
            target = cot_own if own else cot_part
        else:
            target = tok.at[a, core] if own else part.at[a]
        return pltpu.make_async_copy(
            arrays[a].at[:, own_cols if own else part_cols], target, load_sem.at[2 * a + int(own)]
        )

    load_gain = pltpu.make_async_copy(gain_hbm, gain, load_sem.at[8])
    for a in (1, 2):
        load(a, False).start()
    for a in (1, 2):
        load(a, True).start()
    for a in (0, 3):
        load(a, False).start()
        load(a, True).start()
    load_gain.start()

    down_at = [lax.rem(y + d, ROWS) * COLUMNS for d in ring_offsets(ROWS)]
    right_at = [lax.rem(x + d, COLUMNS) for d in ring_offsets(COLUMNS)]

    def other_chips():
        for k in range(ROWS):
            for m in range(COLUMNS):
                if k * COLUMNS + m < PEERS:
                    yield down_at[k] + right_at[m]

    def stack_at(i):
        return {
            "seq": 2 * chip + (core if (i + 1) % 2 == 0 else other),
            "head": lax.rem(z + (i + 1) // 2, stacks),
        }

    stack_peers = 2 * stacks - 1
    partner = {"seq": 2 * chip + other, "head": z}
    barrier = pltpu.get_barrier_semaphore()

    def greet(target):
        pl.semaphore_signal(barrier, inc=1, device_id=target, device_id_type=MESH)

    for target in other_chips():
        greet({"seq": 2 * target + core, "head": z})
    for i in range(stack_peers):
        greet(stack_at(i))

    def remote(src, dst, send, recv, device):
        return pltpu.make_async_remote_copy(
            src_ref=src, dst_ref=dst, send_sem=send, recv_sem=recv, device_id=device, device_id_type=MESH
        )

    def to_core(src, dst, at):
        return remote(src, dst, core_send.at[at], core_recv.at[at], partner)

    def exchange(src, dst, s, chunk, send, recv):
        for target in other_chips():
            remote(
                src.at[s, chunk, target], dst.at[s, chunk, chip], send.at[s, chunk], recv.at[s, chunk],
                {"seq": 2 * target + core, "head": z},
            ).start()

    def whole(ref, s, chunk, send, recv):
        span = ref.at[s, chunk, pl.ds(0, PEERS)]
        return remote(span, span, send.at[s, chunk], recv.at[s, chunk], partner)

    def scan_out(s, chunk):
        exchange(state, gathered, s, chunk, go_send, go_recv)
        gathered[s, chunk, chip] = state[s, chunk, chip]

    def scan_back(s, chunk, reverse):
        with jax.named_scope(f"go_wait{s}{chunk}"):
            whole(gathered, s, chunk, go_send, go_recv).wait_recv()
        with jax.named_scope(f"scan{s}{chunk}"):
            so_far = jnp.zeros((piece, HEAD_DIM), F32)
            for p in reversed(range(CHIPS)) if reverse else range(CHIPS):
                scanned[s, chunk, p] = so_far
                so_far = so_far + gathered[s, chunk, p]
        with jax.named_scope(f"back_start{s}{chunk}"):
            exchange(scanned, prefix, s, chunk, back_send, back_recv)
            prefix[s, chunk, chip] = scanned[s, chunk, chip]

    def scan_in(s, chunk):
        with jax.named_scope(f"back_wait{s}{chunk}"):
            whole(prefix, s, chunk, back_send, back_recv).wait_recv()

    def head_of(s, j):
        at = pl.ds(j % per_chunk * per_head, per_head)
        return prefix[s, j // per_chunk, at].reshape(HEAD_DIM, HEAD_DIM)

    def put_state(s, j, value):
        at = pl.ds(j % per_chunk * per_head, per_head)
        state[s, j // per_chunk, at] = value.reshape(per_head, piece, HEAD_DIM)

    def give_states(chunk):
        at = pl.ds(chunk * per_chunk, per_chunk)
        return to_core(state_out.at[at], blocks.at[core, at], chunk)

    def take_states(chunk):
        at = pl.ds(chunk * per_chunk, per_chunk)
        return to_core(state_out.at[at], blocks.at[other, at], chunk)

    def part_states(chunk):
        for j in heads_of(chunk):
            state_out[j] = dot(part[1, :, col(j)], part[2, :, col(j)], (0, 0))

    with jax.named_scope("load_wait"):
        for a in (1, 2):
            load(a, False).wait()
    with jax.named_scope("states_a"):
        part_states(0)
    with jax.named_scope("barrier"):
        pl.semaphore_wait(barrier, PEERS + stack_peers)
    give_states(0).start()
    for chunk in range(1, CHUNKS):
        part_states(chunk)
        give_states(chunk).start()
    with jax.named_scope("states_b"):
        for a in (1, 2):
            load(a, True).wait()
        for j in range(heads):
            blocks[core, j] = dot(tok[1, core, :, col(j)], tok[2, core, :, col(j)], (0, 0))
    for chunk in range(CHUNKS):
        with jax.named_scope(f"core_wait{chunk}"):
            take_states(chunk).wait_recv()
        with jax.named_scope(f"go0{chunk}"):
            for j in heads_of(chunk):
                put_state(0, j, blocks[0, j] + blocks[1, j])
            scan_out(0, chunk)

    def give_tokens(n):
        return to_core(stage.at[n], came.at[n], CHUNKS + n)

    with jax.named_scope("stage"):
        for n, a in enumerate((1, 2, 0)):
            if a == 0:
                load(0, False).wait()
            stage[n] = part[a].astype(F32)
            give_tokens(n).start()
        load(3, False).wait()
        stage[3] = cot_part[...].astype(F32)
        give_tokens(3).start()

    causal = lax.broadcasted_iota(jnp.int32, (tokens, tokens), 0) >= lax.broadcasted_iota(
        jnp.int32, (tokens, tokens), 1
    )

    def masked(product):
        return jnp.where(causal, product * scale, 0.0).astype(BF16)

    def gain_of(j):
        return gain[pl.ds(core * heads + j, 1), :]

    def within_block(b):
        for j in range(heads):
            w = masked(dot(tok[0, b, :, col(j)], tok[1, b, :, col(j)], (1, 1)))
            weights[b, :, col(j)] = w
            attended[b, :, col(j)] = dot(w, tok[2, b, :, col(j)], (1, 0))

    with jax.named_scope("within_own"):
        load(0, True).wait()
        load(3, True).wait()
        load_gain.wait()
        for j in range(heads):
            scaled[core, :, col(j)] = cot_own[:, col(j)].astype(F32) * gain_of(j)
        within_block(core)
    with jax.named_scope("within_other"):
        for n, a in enumerate((1, 2, 0)):
            give_tokens(n).wait_recv()
            tok[a, other] = came[n].astype(BF16)
        give_tokens(3).wait_recv()
        for j in range(heads):
            scaled[other, :, col(j)] = came[3, :, col(j)] * gain_of(j)
        within_block(other)

    for chunk in range(CHUNKS):
        scan_back(0, chunk, False)

    squares = [jnp.zeros((tokens, HEAD_DIM), F32) for _ in range(2)]
    crosses = [jnp.zeros((tokens, HEAD_DIM), F32) for _ in range(2)]
    for chunk in range(CHUNKS):
        scan_in(0, chunk)
        with jax.named_scope(f"attended{chunk}"):
            for j in heads_of(chunk):
                before = head_of(0, j)
                low[0, j] = before.astype(BF16)
                low[1, j] = (before + blocks[0, j]).astype(BF16)
                for b in range(2):
                    att = attended[b, :, col(j)] + scale * dot(tok[0, b, :, col(j)], low[b, j], (1, 0))
                    attended[b, :, col(j)] = att
                    squares[b] = squares[b] + att * att
                    crosses[b] = crosses[b] + att * scaled[b, :, col(j)]
    me = 2 * z + core
    with jax.named_scope("statsum"):
        for r, sums in enumerate(squares + crosses):
            stats[me, pl.ds(r, 1), :] = jnp.sum(sums.T, axis=0, keepdims=True)
        for i in range(stack_peers):
            remote(stats.at[me], stats.at[me], stat_send, stat_recv, stack_at(i)).start()
    rest = stats.at[pl.ds(0, stack_peers)]
    all_stats = remote(rest, rest, stat_send, stat_recv, partner)
    with jax.named_scope("stat_wait"):
        all_stats.wait_recv()
    with jax.named_scope("stat_use"):
        total = stats[0]
        for p in range(1, 2 * stacks):
            total = total + stats[p]
        inverse_rms = lax.rsqrt(total[0:2] / width + EPSILON)
        cross_mean = total[2:4] * inverse_rms / width

        def down(row):
            return jnp.broadcast_to(row, (HEAD_DIM, tokens)).T

        inverse = [down(inverse_rms[b : b + 1]) for b in range(2)]
        cross = [down(cross_mean[b : b + 1]) for b in range(2)]
    for chunk in range(CHUNKS):
        with jax.named_scope(f"grads{chunk}"):
            for j in heads_of(chunk):
                sums = []
                for b in range(2):
                    normed = attended[b, :, col(j)] * inverse[b]
                    grad = ((scaled[b, :, col(j)] - normed * cross[b]) * inverse[b]).astype(BF16)
                    grads[b, :, col(j)] = grad
                    sums.append(dot(tok[0, b, :, col(j)], grad, (0, 0)))
                late[j] = sums[1]
                put_state(1, j, sums[0] + sums[1])
        with jax.named_scope(f"go1{chunk}"):
            scan_out(1, chunk)

    def without_suffix(b):
        for j in range(heads):
            grad = grads[b, :, col(j)]
            gw = masked(dot(grad, tok[2, b, :, col(j)], (1, 1)))
            grad_f32[0, b, :, col(j)] = dot(gw, tok[1, b, :, col(j)], (1, 0)) + scale * dot(
                grad, low[b, j], (1, 1)
            )
            grad_f32[1, b, :, col(j)] = dot(gw, tok[0, b, :, col(j)], (0, 0))
            grad_f32[2, b, :, col(j)] = dot(weights[b, :, col(j)], grad, (0, 0))

    base = CHUNKS + 4
    give_query = to_core(grad_f32.at[0, other], grad_came.at[0], base)

    def give(n, chunk):
        at = pl.ds(chunk * per_chunk * HEAD_DIM, per_chunk * HEAD_DIM)
        return to_core(grad_f32.at[n, other, :, at], grad_came.at[n, :, at], base + 1 + 2 * chunk + n - 1)

    with jax.named_scope("without_suffix"):
        without_suffix(other)
        give_query.start()
        without_suffix(core)
        result[0, :, own_cols] = grad_f32[0, core].astype(BF16)
    with jax.named_scope("dq_out"):
        give_query.wait_recv()
        result[0, :, part_cols] = grad_came[0].astype(BF16)

    for chunk in range(CHUNKS):
        scan_back(1, chunk, True)

    def with_suffix(b, j, suffix):
        grad_f32[1, b, :, col(j)] += scale * dot(tok[2, b, :, col(j)], suffix, (1, 1))
        grad_f32[2, b, :, col(j)] += scale * dot(tok[1, b, :, col(j)], suffix, (1, 0))

    for chunk in range(CHUNKS):
        scan_in(1, chunk)
        with jax.named_scope(f"with_suffix{chunk}"):
            for j in heads_of(chunk):
                after = head_of(1, j)
                with_suffix(0, j, (after + late[j]).astype(BF16))
                with_suffix(1, j, after.astype(BF16))
            for n in (1, 2):
                give(n, chunk).start()
    with jax.named_scope("own_out"):
        for n in (1, 2):
            result[n, :, own_cols] = grad_f32[n, core].astype(BF16)

    with jax.named_scope("send_waits"):
        for chunk in range(CHUNKS):
            give_states(chunk).wait_send()
        for n in range(4):
            give_tokens(n).wait_send()
        for s in range(2):
            for chunk in range(CHUNKS):
                whole(state, s, chunk, go_send, go_recv).wait_send()
                whole(scanned, s, chunk, back_send, back_recv).wait_send()
        all_stats.wait_send()
        give_query.wait_send()
    with jax.named_scope("final_core"):
        for chunk in range(CHUNKS):
            for n in (1, 2):
                give(n, chunk).wait_recv()
        for n in (1, 2):
            result[n, :, part_cols] = grad_came[n].astype(BF16)
        for chunk in range(CHUNKS):
            for n in (1, 2):
                give(n, chunk).wait_send()


def write_out(result, dq_hbm, dk_hbm, dv_hbm, sems):
    copies = [
        pltpu.make_async_copy(result.at[n], out, sems.at[n]) for n, out in enumerate((dq_hbm, dk_hbm, dv_hbm))
    ]
    for copy in copies:
        copy.start()
    for copy in copies:
        copy.wait()


def per_device(stacks, queries, keys, values, cotangent, gain):
    tokens, local = queries.shape
    mine = local // 2
    heads = mine // HEAD_DIM
    piece = heads * HEAD_DIM // CHIPS // CHUNKS
    anywhere = pl.BlockSpec(memory_space=pl.ANY)
    vmem = pl.BlockSpec(memory_space=pltpu.VMEM)
    dma = pltpu.SemaphoreType.DMA
    arrays = (queries, keys, values, cotangent, gain.reshape(2 * heads, HEAD_DIM))
    result = pl.pallas_call(
        functools.partial(kernel, stacks, mine),
        out_shape=jax.ShapeDtypeStruct((3, tokens, local), BF16),
        in_specs=[pl.BlockSpec(memory_space=pltpu.HBM)] * 5,
        out_specs=vmem,
        scratch_shapes=[
            pltpu.VMEM((2 * heads, HEAD_DIM), F32),
            pltpu.VMEM((3, 2, tokens, mine), BF16),
            pltpu.VMEM((3, tokens, mine), BF16),
            pltpu.VMEM((tokens, mine), BF16),
            pltpu.VMEM((tokens, mine), BF16),
            pltpu.VMEM((4, tokens, mine), F32),
            pltpu.VMEM((4, tokens, mine), F32),
            pltpu.VMEM((2, tokens, mine), F32),
            pltpu.VMEM((2, heads, HEAD_DIM, HEAD_DIM), F32),
            pltpu.VMEM((heads, HEAD_DIM, HEAD_DIM), F32),
            pltpu.VMEM((2, CHUNKS, CHIPS, piece, HEAD_DIM), F32),
            pltpu.VMEM((2, CHUNKS, CHIPS, piece, HEAD_DIM), F32),
            pltpu.VMEM((2, CHUNKS, CHIPS, piece, HEAD_DIM), F32),
            pltpu.VMEM((2, CHUNKS, CHIPS, piece, HEAD_DIM), F32),
            pltpu.VMEM((2, heads, HEAD_DIM, HEAD_DIM), BF16),
            pltpu.VMEM((2, tokens, mine), BF16),
            pltpu.VMEM((2, tokens, mine), F32),
            pltpu.VMEM((2 * stacks, 4, tokens), F32),
            pltpu.VMEM((2, tokens, mine), BF16),
            pltpu.VMEM((heads, HEAD_DIM, HEAD_DIM), F32),
            pltpu.VMEM((3, 2, tokens, mine), F32),
            pltpu.VMEM((3, tokens, mine), F32),
            dma((9,)),
            dma((5 + 3 * CHUNKS,)), dma((5 + 3 * CHUNKS,)),
            dma((2, CHUNKS)), dma((2, CHUNKS)), dma((2, CHUNKS)), dma((2, CHUNKS)),
            dma, dma,
        ],
        compiler_params=pltpu.CompilerParams(
            collective_id=0, has_side_effects=True, vmem_limit_bytes=24 * 1024 * 1024
        ),
        name="attention",
    )(*(pltpu.with_memory_space_constraint(a, pltpu.HBM) for a in arrays))
    out = jax.ShapeDtypeStruct((tokens, local), BF16)
    return pl.pallas_call(
        write_out,
        out_shape=(out, out, out),
        in_specs=[vmem],
        out_specs=(anywhere,) * 3,
        scratch_shapes=[dma((3,))],
        compiler_params=pltpu.CompilerParams(vmem_limit_bytes=4 * 1024 * 1024),
        name="write_out",
    )(result)


def solution(mesh):
    spec = P("seq", "head")
    return jax.shard_map(
        functools.partial(per_device, mesh.shape["head"]),
        mesh=mesh,
        in_specs=(spec, spec, spec, spec, P("head")),
        out_specs=(spec, spec, spec),
        check_vma=False,
    )
```

time: 70.2 us -> 57.8 us (0.82)
  Pallas kernels: 65.9 us -> 57 us
  local copies, waits for them, and re-layouts: 3.46 us -> 0 us
    pallas_call x1 -> x2, Pallas kernels: 65.9 us -> 57 us  [the longest x1 56.1 us: per_device(): pl.pallas_call(functools.partial(kernel, stacks, mine), out_shape=jax.Sha...]
    unnamed x7 -> x0, local copies, waits for them, and re-layouts: 3.46 us -> none
where the time goes in v2:
time: 57.8 us; the launch traced here: 57.7 us
  Pallas kernels  57 us (99%)
  between operations  0.64 us (1%)
    pallas_call x1, Pallas kernels, per_device(): pl.pallas_call(functools.partial(kernel, stacks, mine), out_shape=jax.Sha...  56.1 us

profile of v2, /device:TPU:1, one launch (start us, length us, event | category | flops | bytes accessed | tf_op | source)
XLA Modules:
  0.0 57.7 jit_solution(8023534233355258907)
XLA Ops:
  0.6 56.1 %attention.1.result = bf16[3,128,1024]{2,1,0:T(8,128)(2,1)S(1)} custom-call(bf16[128,1024]{1,0:T(8,128)(2,1)} %q_hbm.1, bf16[128,1024]{1,0:T(8,128)(2,1)} %k_hbm.1, bf16[128,1024]{1,0:T(8,128)(2,1)} %v_hbm.1, bf16[128,1024]{1,0:T(8,128)(2,1)} %cot_hbm.1, f32[8,128]{1,0:T(8,128)} %bitcast.1), custom_call_target="tpu_custom_call" | custom-call | tf_op jit(solution)/shard_map/attention/pallas_call | solution.py:376
  56.8 0.9 %write_out.1 = (bf16[128,1024]{1,0:T(8,128)(2,1)}, bf16[128,1024]{1,0:T(8,128)(2,1)}, bf16[128,1024]{1,0:T(8,128)(2,1)}) custom-call(bf16[3,128,1024]{2,1,0:T(8,128)(2,1)S(1)} %attention.1.result), custom_call_target="tpu_custom_call" | custom-call | tf_op jit(solution)/shard_map/write_out/pallas_call | solution.py:415

commit v3 on v2

--- a/solution.py
+++ b/solution.py
@@ -11,7 +11,6 @@
 EPSILON = 1e-05
 ROWS, COLUMNS = 8, 4
 CHIPS = ROWS * COLUMNS
-PEERS = CHIPS - 1
 CHUNKS = 2
 MESH = pl.DeviceIdType.MESH
 F32, BF16 = jnp.float32, jnp.bfloat16
@@ -34,6 +33,7 @@
     weights, attended, stats, grads, late,
     grad_f32, grad_came,
     load_sem, core_send, core_recv, go_send, go_recv, back_send, back_recv, stat_send, stat_recv,
+    met, stack_ready,
 ):
     seq, z = lax.axis_index("seq"), lax.axis_index("head")
     core = lax.rem(seq, 2)
@@ -69,41 +69,80 @@
         )
 
     load_gain = pltpu.make_async_copy(gain_hbm, gain, load_sem.at[8])
-    for a in (1, 2):
-        load(a, False).start()
-    for a in (1, 2):
-        load(a, True).start()
-    for a in (0, 3):
-        load(a, False).start()
-        load(a, True).start()
-    load_gain.start()
+    with jax.named_scope("load_first"):
+        for a in (1, 2):
+            load(a, False).start()
 
     down_at = [lax.rem(y + d, ROWS) * COLUMNS for d in ring_offsets(ROWS)]
     right_at = [lax.rem(x + d, COLUMNS) for d in ring_offsets(COLUMNS)]
-
-    def other_chips():
-        for k in range(ROWS):
-            for m in range(COLUMNS):
-                if k * COLUMNS + m < PEERS:
-                    yield down_at[k] + right_at[m]
-
-    def stack_at(i):
-        return {
-            "seq": 2 * chip + (core if (i + 1) % 2 == 0 else other),
-            "head": lax.rem(z + (i + 1) // 2, stacks),
-        }
-
-    stack_peers = 2 * stacks - 1
+    offsets = [(d, r) for d in range(ROWS) for r in range(COLUMNS)]
+    all_chips = [down_at[d] + right_at[r] for d, r in offsets]
+    odd = [(ring_offsets(ROWS)[d] + ring_offsets(COLUMNS)[r]) % 2 for d, r in offsets]
+    colour = lax.rem(x + y, 2)
+
+    def place(target, its_colour):
+        return its_colour * (CHIPS // 2) + lax.div(target, 2)
+
+    my_place = place(chip, colour)
+
+    def owners(wanted):
+        for target, is_odd in zip(all_chips, odd):
+            if is_odd == wanted:
+                yield target
+
     partner = {"seq": 2 * chip + other, "head": z}
     barrier = pltpu.get_barrier_semaphore()
 
-    def greet(target):
-        pl.semaphore_signal(barrier, inc=1, device_id=target, device_id_type=MESH)
-
-    for target in other_chips():
-        greet({"seq": 2 * target + core, "head": z})
-    for i in range(stack_peers):
-        greet(stack_at(i))
+    def tell(sem, target):
+        pl.semaphore_signal(sem, inc=1, device_id=target, device_id_type=MESH)
+
+    with jax.named_scope("greet"):
+        for target in all_chips[:-1]:
+            tell(barrier, {"seq": 2 * target + 1, "head": z})
+
+        @pl.when(core == 1)
+        def _():
+            tell(barrier, partner)
+
+        for plane in range(1, stacks):
+
+            @pl.when(plane > z)
+            def _():
+                tell(barrier, {"seq": 2 * chip + 1, "head": plane})
+
+    def meet_partner():
+        @pl.when(core == 0)
+        def _():
+            pl.semaphore_wait(barrier, 1)
+            tell(met, partner)
+
+        @pl.when(core == 1)
+        def _():
+            pl.semaphore_wait(met, 1)
+
+    def meet_plane():
+        @pl.when(core == 1)
+        def _():
+            pl.semaphore_wait(barrier, 2 * (CHIPS - 1) + 2 * z)
+            tell(met, partner)
+            for plane in range(stacks - 1):
+
+                @pl.when(plane < z)
+                def _():
+                    tell(stack_ready, {"seq": 2 * chip, "head": plane})
+                    tell(stack_ready, {"seq": 2 * chip + 1, "head": plane})
+
+        @pl.when(core == 0)
+        def _():
+            pl.semaphore_wait(met, 1)
+
+    with jax.named_scope("load_rest"):
+        for a in (1, 2):
+            load(a, True).start()
+        for a in (0, 3):
+            load(a, False).start()
+            load(a, True).start()
+        load_gain.start()
 
     def remote(src, dst, send, recv, device):
         return pltpu.make_async_remote_copy(
@@ -113,36 +152,44 @@
     def to_core(src, dst, at):
         return remote(src, dst, core_send.at[at], core_recv.at[at], partner)
 
-    def exchange(src, dst, s, chunk, send, recv):
-        for target in other_chips():
+    def go(s, chunk):
+        for first in range(2):
+
+            @pl.when(colour == first)
+            def _():
+                for head in range(2):
+                    for target in owners((head + first) % 2):
+                        remote(
+                            state.at[s, chunk, place(target, head)], gathered.at[s, chunk, chip],
+                            go_send.at[s, chunk], go_recv.at[s, chunk], {"seq": 2 * target + other, "head": z},
+                        ).start()
+
+    def back(s, chunk):
+        for target in all_chips:
             remote(
-                src.at[s, chunk, target], dst.at[s, chunk, chip], send.at[s, chunk], recv.at[s, chunk],
-                {"seq": 2 * target + core, "head": z},
+                scanned.at[s, chunk, target], prefix.at[s, chunk, my_place],
+                back_send.at[s, chunk], back_recv.at[s, chunk, colour], {"seq": 2 * target + other, "head": z},
             ).start()
 
     def whole(ref, s, chunk, send, recv):
-        span = ref.at[s, chunk, pl.ds(0, PEERS)]
-        return remote(span, span, send.at[s, chunk], recv.at[s, chunk], partner)
-
-    def scan_out(s, chunk):
-        exchange(state, gathered, s, chunk, go_send, go_recv)
-        gathered[s, chunk, chip] = state[s, chunk, chip]
+        span = ref.at[s, chunk]
+        return remote(span, span, send.at[s, chunk], recv, partner)
 
     def scan_back(s, chunk, reverse):
         with jax.named_scope(f"go_wait{s}{chunk}"):
-            whole(gathered, s, chunk, go_send, go_recv).wait_recv()
+            whole(gathered, s, chunk, go_send, go_recv.at[s, chunk]).wait_recv()
         with jax.named_scope(f"scan{s}{chunk}"):
             so_far = jnp.zeros((piece, HEAD_DIM), F32)
             for p in reversed(range(CHIPS)) if reverse else range(CHIPS):
                 scanned[s, chunk, p] = so_far
                 so_far = so_far + gathered[s, chunk, p]
         with jax.named_scope(f"back_start{s}{chunk}"):
-            exchange(scanned, prefix, s, chunk, back_send, back_recv)
-            prefix[s, chunk, chip] = scanned[s, chunk, chip]
-
-    def scan_in(s, chunk):
-        with jax.named_scope(f"back_wait{s}{chunk}"):
-            whole(prefix, s, chunk, back_send, back_recv).wait_recv()
+            back(s, chunk)
+
+    def scan_in(s, j):
+        half = prefix.at[s, j // 2, pl.ds(j % 2 * (CHIPS // 2), CHIPS // 2)]
+        with jax.named_scope(f"back_wait{s}{j}"):
+            remote(half, half, back_send.at[s, j // 2], back_recv.at[s, j // 2, j % 2], partner).wait_recv()
 
     def head_of(s, j):
         at = pl.ds(j % per_chunk * per_head, per_head)
@@ -169,8 +216,8 @@
             load(a, False).wait()
     with jax.named_scope("states_a"):
         part_states(0)
-    with jax.named_scope("barrier"):
-        pl.semaphore_wait(barrier, PEERS + stack_peers)
+    with jax.named_scope("meet_partner"):
+        meet_partner()
     give_states(0).start()
     for chunk in range(1, CHUNKS):
         part_states(chunk)
@@ -180,13 +227,16 @@
             load(a, True).wait()
         for j in range(heads):
             blocks[core, j] = dot(tok[1, core, :, col(j)], tok[2, core, :, col(j)], (0, 0))
-    for chunk in range(CHUNKS):
-        with jax.named_scope(f"core_wait{chunk}"):
+    with jax.named_scope("core_wait"):
+        for chunk in range(CHUNKS):
             take_states(chunk).wait_recv()
-        with jax.named_scope(f"go0{chunk}"):
             for j in heads_of(chunk):
                 put_state(0, j, blocks[0, j] + blocks[1, j])
-            scan_out(0, chunk)
+    with jax.named_scope("barrier"):
+        meet_plane()
+    for chunk in range(CHUNKS):
+        with jax.named_scope(f"go0{chunk}"):
+            go(0, chunk)
 
     def give_tokens(n):
         return to_core(stage.at[n], came.at[n], CHUNKS + n)
@@ -238,10 +288,10 @@
 
     squares = [jnp.zeros((tokens, HEAD_DIM), F32) for _ in range(2)]
     crosses = [jnp.zeros((tokens, HEAD_DIM), F32) for _ in range(2)]
-    for chunk in range(CHUNKS):
-        scan_in(0, chunk)
-        with jax.named_scope(f"attended{chunk}"):
-            for j in heads_of(chunk):
+    for head in range(heads):
+        scan_in(0, head)
+        with jax.named_scope(f"attended{head}"):
+            for j in (head,):
                 before = head_of(0, j)
                 low[0, j] = before.astype(BF16)
                 low[1, j] = (before + blocks[0, j]).astype(BF16)
@@ -254,9 +304,16 @@
     with jax.named_scope("statsum"):
         for r, sums in enumerate(squares + crosses):
             stats[me, pl.ds(r, 1), :] = jnp.sum(sums.T, axis=0, keepdims=True)
-        for i in range(stack_peers):
-            remote(stats.at[me], stats.at[me], stat_send, stat_recv, stack_at(i)).start()
-    rest = stats.at[pl.ds(0, stack_peers)]
+        @pl.when(z < stacks - 1)
+        def _():
+            pl.semaphore_wait(stack_ready, stacks - 1 - z)
+
+        for up in range(1, stacks):
+            for there in (core, other):
+                device = {"seq": 2 * chip + there, "head": lax.rem(z + up, stacks)}
+                remote(stats.at[me], stats.at[me], stat_send, stat_recv, device).start()
+        remote(stats.at[me], stats.at[me], stat_send, stat_recv, partner).start()
+    rest = stats.at[pl.ds(0, 2 * stacks - 1)]
     all_stats = remote(rest, rest, stat_send, stat_recv, partner)
     with jax.named_scope("stat_wait"):
         all_stats.wait_recv()
@@ -284,7 +341,7 @@
                 late[j] = sums[1]
                 put_state(1, j, sums[0] + sums[1])
         with jax.named_scope(f"go1{chunk}"):
-            scan_out(1, chunk)
+            go(1, chunk)
 
     def without_suffix(b):
         for j in range(heads):
@@ -299,9 +356,8 @@
     base = CHUNKS + 4
     give_query = to_core(grad_f32.at[0, other], grad_came.at[0], base)
 
-    def give(n, chunk):
-        at = pl.ds(chunk * per_chunk * HEAD_DIM, per_chunk * HEAD_DIM)
-        return to_core(grad_f32.at[n, other, :, at], grad_came.at[n, :, at], base + 1 + 2 * chunk + n - 1)
+    def give(n, j):
+        return to_core(grad_f32.at[n, other, :, col(j)], grad_came.at[n, :, col(j)], base + 2 * j + n)
 
     with jax.named_scope("without_suffix"):
         without_suffix(other)
@@ -319,15 +375,14 @@
         grad_f32[1, b, :, col(j)] += scale * dot(tok[2, b, :, col(j)], suffix, (1, 1))
         grad_f32[2, b, :, col(j)] += scale * dot(tok[1, b, :, col(j)], suffix, (1, 0))
 
-    for chunk in range(CHUNKS):
-        scan_in(1, chunk)
-        with jax.named_scope(f"with_suffix{chunk}"):
-            for j in heads_of(chunk):
-                after = head_of(1, j)
-                with_suffix(0, j, (after + late[j]).astype(BF16))
-                with_suffix(1, j, after.astype(BF16))
+    for j in range(heads):
+        scan_in(1, j)
+        with jax.named_scope(f"with_suffix{j}"):
+            after = head_of(1, j)
+            with_suffix(0, j, (after + late[j]).astype(BF16))
+            with_suffix(1, j, after.astype(BF16))
             for n in (1, 2):
-                give(n, chunk).start()
+                give(n, j).start()
     with jax.named_scope("own_out"):
         for n in (1, 2):
             result[n, :, own_cols] = grad_f32[n, core].astype(BF16)
@@ -339,19 +394,19 @@
             give_tokens(n).wait_send()
         for s in range(2):
             for chunk in range(CHUNKS):
-                whole(state, s, chunk, go_send, go_recv).wait_send()
-                whole(scanned, s, chunk, back_send, back_recv).wait_send()
+                whole(state, s, chunk, go_send, go_recv.at[s, chunk]).wait_send()
+                whole(scanned, s, chunk, back_send, go_recv.at[s, chunk]).wait_send()
         all_stats.wait_send()
         give_query.wait_send()
     with jax.named_scope("final_core"):
-        for chunk in range(CHUNKS):
+        for j in range(heads):
             for n in (1, 2):
-                give(n, chunk).wait_recv()
+                give(n, j).wait_recv()
         for n in (1, 2):
             result[n, :, part_cols] = grad_came[n].astype(BF16)
-        for chunk in range(CHUNKS):
+        for j in range(heads):
             for n in (1, 2):
-                give(n, chunk).wait_send()
+                give(n, j).wait_send()
 
 
 def write_out(result, dq_hbm, dk_hbm, dv_hbm, sems):
@@ -402,9 +457,10 @@
             pltpu.VMEM((3, 2, tokens, mine), F32),
             pltpu.VMEM((3, tokens, mine), F32),
             dma((9,)),
-            dma((5 + 3 * CHUNKS,)), dma((5 + 3 * CHUNKS,)),
-            dma((2, CHUNKS)), dma((2, CHUNKS)), dma((2, CHUNKS)), dma((2, CHUNKS)),
+            dma((5 + CHUNKS + 2 * heads,)), dma((5 + CHUNKS + 2 * heads,)),
+            dma((2, CHUNKS)), dma((2, CHUNKS)), dma((2, CHUNKS)), dma((2, CHUNKS, 2)),
             dma, dma,
+            pltpu.SemaphoreType.REGULAR, pltpu.SemaphoreType.REGULAR,
         ],
         compiler_params=pltpu.CompilerParams(
             collective_id=0, has_side_effects=True, vmem_limit_bytes=24 * 1024 * 1024

time: 57.8 us -> 56.3 us (0.974)
  Pallas kernels: 57 us -> 55.5 us
    pallas_call x1, Pallas kernels: 56.1 us -> 54.6 us  [per_device(): pl.pallas_call(functools.partial(kernel, stacks, mine), out_shape=jax.Sha...]
where the time goes in v3:
time: 56.3 us; the launch traced here: 56.1 us
  Pallas kernels  55.5 us (99%)
  between operations  0.64 us (1%)
    pallas_call x1, Pallas kernels, per_device(): pl.pallas_call(functools.partial(kernel, stacks, mine), out_shape=jax.Sha...  54.6 us

profile of v3, /device:TPU:1, one launch (start us, length us, event | category | flops | bytes accessed | tf_op | source)
XLA Modules:
  0.0 56.1 jit_solution(2284105670686618694)
XLA Ops:
  0.6 54.6 %attention.1.result = bf16[3,128,1024]{2,1,0:T(8,128)(2,1)S(1)} custom-call(bf16[128,1024]{1,0:T(8,128)(2,1)} %q_hbm.1, bf16[128,1024]{1,0:T(8,128)(2,1)} %k_hbm.1, bf16[128,1024]{1,0:T(8,128)(2,1)} %v_hbm.1, bf16[128,1024]{1,0:T(8,128)(2,1)} %cot_hbm.1, f32[8,128]{1,0:T(8,128)} %bitcast.1), custom_call_target="tpu_custom_call" | custom-call | tf_op jit(solution)/shard_map/attention/pallas_call | solution.py:431
  55.2 0.9 %write_out.1 = (bf16[128,1024]{1,0:T(8,128)(2,1)}, bf16[128,1024]{1,0:T(8,128)(2,1)}, bf16[128,1024]{1,0:T(8,128)(2,1)}) custom-call(bf16[3,128,1024]{2,1,0:T(8,128)(2,1)S(1)} %attention.1.result), custom_call_target="tpu_custom_call" | custom-call | tf_op jit(solution)/shard_map/write_out/pallas_call | solution.py:471

commit v4 on v3

--- a/solution.py
+++ b/solution.py
@@ -149,8 +149,8 @@
             src_ref=src, dst_ref=dst, send_sem=send, recv_sem=recv, device_id=device, device_id_type=MESH
         )
 
-    def to_core(src, dst, at):
-        return remote(src, dst, core_send.at[at], core_recv.at[at], partner)
+    def to_core(src, dst, sent, received):
+        return remote(src, dst, core_send.at[sent], core_recv.at[received], partner)
 
     def go(s, chunk):
         for first in range(2):
@@ -161,23 +161,19 @@
                     for target in owners((head + first) % 2):
                         remote(
                             state.at[s, chunk, place(target, head)], gathered.at[s, chunk, chip],
-                            go_send.at[s, chunk], go_recv.at[s, chunk], {"seq": 2 * target + other, "head": z},
+                            go_send, go_recv.at[s, chunk], {"seq": 2 * target + other, "head": z},
                         ).start()
 
     def back(s, chunk):
         for target in all_chips:
             remote(
                 scanned.at[s, chunk, target], prefix.at[s, chunk, my_place],
-                back_send.at[s, chunk], back_recv.at[s, chunk, colour], {"seq": 2 * target + other, "head": z},
+                back_send, back_recv.at[s, chunk, colour], {"seq": 2 * target + other, "head": z},
             ).start()
-
-    def whole(ref, s, chunk, send, recv):
-        span = ref.at[s, chunk]
-        return remote(span, span, send.at[s, chunk], recv, partner)
 
     def scan_back(s, chunk, reverse):
         with jax.named_scope(f"go_wait{s}{chunk}"):
-            whole(gathered, s, chunk, go_send, go_recv.at[s, chunk]).wait_recv()
+            remote(gathered.at[s, chunk], gathered.at[s, chunk], go_send, go_recv.at[s, chunk], partner).wait_recv()
         with jax.named_scope(f"scan{s}{chunk}"):
             so_far = jnp.zeros((piece, HEAD_DIM), F32)
             for p in reversed(range(CHIPS)) if reverse else range(CHIPS):
@@ -189,7 +185,7 @@
     def scan_in(s, j):
         half = prefix.at[s, j // 2, pl.ds(j % 2 * (CHIPS // 2), CHIPS // 2)]
         with jax.named_scope(f"back_wait{s}{j}"):
-            remote(half, half, back_send.at[s, j // 2], back_recv.at[s, j // 2, j % 2], partner).wait_recv()
+            remote(half, half, back_send, back_recv.at[s, j // 2, j % 2], partner).wait_recv()
 
     def head_of(s, j):
         at = pl.ds(j % per_chunk * per_head, per_head)
@@ -201,11 +197,11 @@
 
     def give_states(chunk):
         at = pl.ds(chunk * per_chunk, per_chunk)
-        return to_core(state_out.at[at], blocks.at[core, at], chunk)
+        return to_core(state_out.at[at], blocks.at[core, at], 0, chunk)
 
     def take_states(chunk):
         at = pl.ds(chunk * per_chunk, per_chunk)
-        return to_core(state_out.at[at], blocks.at[other, at], chunk)
+        return to_core(state_out.at[at], blocks.at[other, at], 0, chunk)
 
     def part_states(chunk):
         for j in heads_of(chunk):
@@ -238,8 +234,31 @@
         with jax.named_scope(f"go0{chunk}"):
             go(0, chunk)
 
+    causal = lax.broadcasted_iota(jnp.int32, (tokens, tokens), 0) >= lax.broadcasted_iota(
+        jnp.int32, (tokens, tokens), 1
+    )
+
+    def masked(product):
+        return jnp.where(causal, product * scale, 0.0).astype(BF16)
+
+    def gain_of(j):
+        return gain[pl.ds(core * heads + j, 1), :]
+
+    def within_block(b):
+        for j in range(heads):
+            w = masked(dot(tok[0, b, :, col(j)], tok[1, b, :, col(j)], (1, 1)))
+            weights[b, :, col(j)] = w
+            attended[b, :, col(j)] = dot(w, tok[2, b, :, col(j)], (1, 0))
+
+    with jax.named_scope("within_own"):
+        load(0, True).wait()
+        load(3, True).wait()
+        load_gain.wait()
+        for j in range(heads):
+            scaled[core, :, col(j)] = cot_own[:, col(j)].astype(F32) * gain_of(j)
+        within_block(core)
     def give_tokens(n):
-        return to_core(stage.at[n], came.at[n], CHUNKS + n)
+        return to_core(stage.at[n], came.at[n], 1, CHUNKS)
 
     with jax.named_scope("stage"):
         for n, a in enumerate((1, 2, 0)):
@@ -251,40 +270,17 @@
         stage[3] = cot_part[...].astype(F32)
         give_tokens(3).start()
 
-    causal = lax.broadcasted_iota(jnp.int32, (tokens, tokens), 0) >= lax.broadcasted_iota(
-        jnp.int32, (tokens, tokens), 1
-    )
-
-    def masked(product):
-        return jnp.where(causal, product * scale, 0.0).astype(BF16)
-
-    def gain_of(j):
-        return gain[pl.ds(core * heads + j, 1), :]
-
-    def within_block(b):
-        for j in range(heads):
-            w = masked(dot(tok[0, b, :, col(j)], tok[1, b, :, col(j)], (1, 1)))
-            weights[b, :, col(j)] = w
-            attended[b, :, col(j)] = dot(w, tok[2, b, :, col(j)], (1, 0))
-
-    with jax.named_scope("within_own"):
-        load(0, True).wait()
-        load(3, True).wait()
-        load_gain.wait()
-        for j in range(heads):
-            scaled[core, :, col(j)] = cot_own[:, col(j)].astype(F32) * gain_of(j)
-        within_block(core)
+    for chunk in range(CHUNKS):
+        scan_back(0, chunk, False)
+
     with jax.named_scope("within_other"):
+        to_core(stage, came, 1, CHUNKS).wait_recv()
         for n, a in enumerate((1, 2, 0)):
-            give_tokens(n).wait_recv()
             tok[a, other] = came[n].astype(BF16)
-        give_tokens(3).wait_recv()
         for j in range(heads):
             scaled[other, :, col(j)] = came[3, :, col(j)] * gain_of(j)
         within_block(other)
 
-    for chunk in range(CHUNKS):
-        scan_back(0, chunk, False)
 
     squares = [jnp.zeros((tokens, HEAD_DIM), F32) for _ in range(2)]
     crosses = [jnp.zeros((tokens, HEAD_DIM), F32) for _ in range(2)]
@@ -353,11 +349,10 @@
             grad_f32[1, b, :, col(j)] = dot(gw, tok[0, b, :, col(j)], (0, 0))
             grad_f32[2, b, :, col(j)] = dot(weights[b, :, col(j)], grad, (0, 0))
 
-    base = CHUNKS + 4
-    give_query = to_core(grad_f32.at[0, other], grad_came.at[0], base)
+    give_query = to_core(grad_f32.at[0, other], grad_came.at[0], 2, CHUNKS + 1)
 
     def give(n, j):
-        return to_core(grad_f32.at[n, other, :, col(j)], grad_came.at[n, :, col(j)], base + 2 * j + n)
+        return to_core(grad_f32.at[n, other, :, col(j)], grad_came.at[n, :, col(j)], 2, CHUNKS + 2)
 
     with jax.named_scope("without_suffix"):
         without_suffix(other)
@@ -388,25 +383,17 @@
             result[n, :, own_cols] = grad_f32[n, core].astype(BF16)
 
     with jax.named_scope("send_waits"):
-        for chunk in range(CHUNKS):
-            give_states(chunk).wait_send()
-        for n in range(4):
-            give_tokens(n).wait_send()
-        for s in range(2):
-            for chunk in range(CHUNKS):
-                whole(state, s, chunk, go_send, go_recv.at[s, chunk]).wait_send()
-                whole(scanned, s, chunk, back_send, go_recv.at[s, chunk]).wait_send()
+        to_core(state_out, state_out, 0, 0).wait_send()
+        to_core(stage, stage, 1, 0).wait_send()
+        remote(state, state, go_send, go_recv.at[0, 0], partner).wait_send()
+        remote(scanned, scanned, back_send, go_recv.at[0, 0], partner).wait_send()
         all_stats.wait_send()
-        give_query.wait_send()
     with jax.named_scope("final_core"):
-        for j in range(heads):
-            for n in (1, 2):
-                give(n, j).wait_recv()
+        keys_values = grad_came.at[pl.ds(1, 2)]
+        to_core(keys_values, keys_values, 2, CHUNKS + 2).wait_recv()
         for n in (1, 2):
             result[n, :, part_cols] = grad_came[n].astype(BF16)
-        for j in range(heads):
-            for n in (1, 2):
-                give(n, j).wait_send()
+        to_core(grad_came, grad_came, 2, 0).wait_send()
 
 
 def write_out(result, dq_hbm, dk_hbm, dv_hbm, sems):
@@ -457,8 +444,8 @@
             pltpu.VMEM((3, 2, tokens, mine), F32),
             pltpu.VMEM((3, tokens, mine), F32),
             dma((9,)),
-            dma((5 + CHUNKS + 2 * heads,)), dma((5 + CHUNKS + 2 * heads,)),
-            dma((2, CHUNKS)), dma((2, CHUNKS)), dma((2, CHUNKS)), dma((2, CHUNKS, 2)),
+            dma((3,)), dma((CHUNKS + 3,)),
+            dma, dma((2, CHUNKS)), dma, dma((2, CHUNKS, 2)),
             dma, dma,
             pltpu.SemaphoreType.REGULAR, pltpu.SemaphoreType.REGULAR,
         ],

time: 56.3 us -> 56 us (level)
  no operation moved by 1% of the time
where the time goes in v4:
time: 56 us; the launch traced here: 55.8 us
  Pallas kernels  55.2 us (99%)
  between operations  0.64 us (1%)
    pallas_call x1, Pallas kernels, per_device(): pl.pallas_call(functools.partial(kernel, stacks, mine), out_shape=jax.Sha...  54.3 us

profile of v4, /device:TPU:1, one launch (start us, length us, event | category | flops | bytes accessed | tf_op | source)
XLA Modules:
  0.0 55.8 jit_solution(9989250022834914538)
XLA Ops:
  0.6 54.3 %attention.1.result = bf16[3,128,1024]{2,1,0:T(8,128)(2,1)S(1)} custom-call(bf16[128,1024]{1,0:T(8,128)(2,1)} %q_hbm.1, bf16[128,1024]{1,0:T(8,128)(2,1)} %k_hbm.1, bf16[128,1024]{1,0:T(8,128)(2,1)} %v_hbm.1, bf16[128,1024]{1,0:T(8,128)(2,1)} %cot_hbm.1, f32[8,128]{1,0:T(8,128)} %bitcast.1), custom_call_target="tpu_custom_call" | custom-call | tf_op jit(solution)/shard_map/attention/pallas_call | solution.py:418
  54.9 0.9 %write_out.1 = (bf16[128,1024]{1,0:T(8,128)(2,1)}, bf16[128,1024]{1,0:T(8,128)(2,1)}, bf16[128,1024]{1,0:T(8,128)(2,1)}) custom-call(bf16[3,128,1024]{2,1,0:T(8,128)(2,1)S(1)} %attention.1.result), custom_call_target="tpu_custom_call" | custom-call | tf_op jit(solution)/shard_map/write_out/pallas_call | solution.py:458

commit v5 on v4

--- a/solution.py
+++ b/solution.py
@@ -12,6 +12,7 @@
 ROWS, COLUMNS = 8, 4
 CHIPS = ROWS * COLUMNS
 CHUNKS = 2
+PARTS = 1
 MESH = pl.DeviceIdType.MESH
 F32, BF16 = jnp.float32, jnp.bfloat16
 
@@ -125,12 +126,6 @@
         def _():
             pl.semaphore_wait(barrier, 2 * (CHIPS - 1) + 2 * z)
             tell(met, partner)
-            for plane in range(stacks - 1):
-
-                @pl.when(plane < z)
-                def _():
-                    tell(stack_ready, {"seq": 2 * chip, "head": plane})
-                    tell(stack_ready, {"seq": 2 * chip + 1, "head": plane})
 
         @pl.when(core == 0)
         def _():
@@ -152,24 +147,32 @@
     def to_core(src, dst, sent, received):
         return remote(src, dst, core_send.at[sent], core_recv.at[received], partner)
 
-    def go(s, chunk):
-        for first in range(2):
-
-            @pl.when(colour == first)
+    def go(s, j):
+        chunk, head = j // 2, j % 2
+        for mine_owns in range(2):
+
+            @pl.when((colour == head) == bool(mine_owns))
             def _():
-                for head in range(2):
-                    for target in owners((head + first) % 2):
-                        remote(
-                            state.at[s, chunk, place(target, head)], gathered.at[s, chunk, chip],
-                            go_send, go_recv.at[s, chunk], {"seq": 2 * target + other, "head": z},
-                        ).start()
+                for target in owners(1 - mine_owns):
+                    remote(
+                        state.at[s, chunk, place(target, head)], gathered.at[s, chunk, chip],
+                        go_send, go_recv.at[s, chunk], {"seq": 2 * target + other, "head": z},
+                    ).start()
 
     def back(s, chunk):
-        for target in all_chips:
+        def to(target):
             remote(
                 scanned.at[s, chunk, target], prefix.at[s, chunk, my_place],
                 back_send, back_recv.at[s, chunk, colour], {"seq": 2 * target + other, "head": z},
             ).start()
+
+        if s == 0:
+            for target in all_chips:
+                to(target)
+        else:
+            to(0 * chip)
+            for target in all_chips:
+                pl.when(target != 0)(functools.partial(to, target))
 
     def scan_back(s, chunk, reverse):
         with jax.named_scope(f"go_wait{s}{chunk}"):
@@ -230,9 +233,18 @@
                 put_state(0, j, blocks[0, j] + blocks[1, j])
     with jax.named_scope("barrier"):
         meet_plane()
-    for chunk in range(CHUNKS):
-        with jax.named_scope(f"go0{chunk}"):
-            go(0, chunk)
+    with jax.named_scope("go0"):
+        for j in range(heads):
+            go(0, j)
+
+    @pl.when(core == 1)
+    def _():
+        for plane in range(stacks - 1):
+
+            @pl.when(plane < z)
+            def _():
+                tell(stack_ready, {"seq": 2 * chip, "head": plane})
+                tell(stack_ready, {"seq": 2 * chip + 1, "head": plane})
 
     causal = lax.broadcasted_iota(jnp.int32, (tokens, tokens), 0) >= lax.broadcasted_iota(
         jnp.int32, (tokens, tokens), 1
@@ -325,19 +337,17 @@
 
         inverse = [down(inverse_rms[b : b + 1]) for b in range(2)]
         cross = [down(cross_mean[b : b + 1]) for b in range(2)]
-    for chunk in range(CHUNKS):
-        with jax.named_scope(f"grads{chunk}"):
-            for j in heads_of(chunk):
-                sums = []
-                for b in range(2):
-                    normed = attended[b, :, col(j)] * inverse[b]
-                    grad = ((scaled[b, :, col(j)] - normed * cross[b]) * inverse[b]).astype(BF16)
-                    grads[b, :, col(j)] = grad
-                    sums.append(dot(tok[0, b, :, col(j)], grad, (0, 0)))
-                late[j] = sums[1]
-                put_state(1, j, sums[0] + sums[1])
-        with jax.named_scope(f"go1{chunk}"):
-            go(1, chunk)
+    for j in range(heads):
+        with jax.named_scope(f"grads{j}"):
+            sums = []
+            for b in range(2):
+                normed = attended[b, :, col(j)] * inverse[b]
+                grad = ((scaled[b, :, col(j)] - normed * cross[b]) * inverse[b]).astype(BF16)
+                grads[b, :, col(j)] = grad
+                sums.append(dot(tok[0, b, :, col(j)], grad, (0, 0)))
+            late[j] = sums[1]
+            put_state(1, j, sums[0] + sums[1])
+            go(1, j)
 
     def without_suffix(b):
         for j in range(heads):
@@ -397,8 +407,13 @@
 
 
 def write_out(result, dq_hbm, dk_hbm, dv_hbm, sems):
+    step = result.shape[1] // PARTS
     copies = [
-        pltpu.make_async_copy(result.at[n], out, sems.at[n]) for n, out in enumerate((dq_hbm, dk_hbm, dv_hbm))
+        pltpu.make_async_copy(
+            result.at[n, pl.ds(p * step, step)], out.at[pl.ds(p * step, step)], sems.at[PARTS * n + p]
+        )
+        for n, out in enumerate((dq_hbm, dk_hbm, dv_hbm))
+        for p in range(PARTS)
     ]
     for copy in copies:
         copy.start()
@@ -460,7 +475,7 @@
         out_shape=(out, out, out),
         in_specs=[vmem],
         out_specs=(anywhere,) * 3,
-        scratch_shapes=[dma((3,))],
+        scratch_shapes=[dma((3 * PARTS,))],
         compiler_params=pltpu.CompilerParams(vmem_limit_bytes=4 * 1024 * 1024),
         name="write_out",
     )(result)

time: 56 us -> 55.3 us (0.987)
  Pallas kernels: 55.2 us -> 54.6 us
    pallas_call x1, Pallas kernels: 54.3 us -> 53.7 us  [per_device(): pl.pallas_call(functools.partial(kernel, stacks, mine), out_shape=jax.Sha...]
where the time goes in v5:
time: 55.3 us; the launch traced here: 55.2 us
  Pallas kernels  54.6 us (99%)
  between operations  0.64 us (1%)
    pallas_call x1, Pallas kernels, per_device(): pl.pallas_call(functools.partial(kernel, stacks, mine), out_shape=jax.Sha...  53.7 us

profile of v5, /device:TPU:1, one launch (start us, length us, event | category | flops | bytes accessed | tf_op | source)
XLA Modules:
  0.0 55.2 jit_solution(5341413739524276694)
XLA Ops:
  0.6 53.7 %attention.1.result = bf16[3,128,1024]{2,1,0:T(8,128)(2,1)S(1)} custom-call(bf16[128,1024]{1,0:T(8,128)(2,1)} %q_hbm.1, bf16[128,1024]{1,0:T(8,128)(2,1)} %k_hbm.1, bf16[128,1024]{1,0:T(8,128)(2,1)} %v_hbm.1, bf16[128,1024]{1,0:T(8,128)(2,1)} %cot_hbm.1, f32[8,128]{1,0:T(8,128)} %bitcast.1), custom_call_target="tpu_custom_call" | custom-call | tf_op jit(solution)/shard_map/attention/pallas_call | solution.py:433
  54.3 0.9 %write_out.1 = (bf16[128,1024]{1,0:T(8,128)(2,1)}, bf16[128,1024]{1,0:T(8,128)(2,1)}, bf16[128,1024]{1,0:T(8,128)(2,1)}) custom-call(bf16[3,128,1024]{2,1,0:T(8,128)(2,1)S(1)} %attention.1.result), custom_call_target="tpu_custom_call" | custom-call | tf_op jit(solution)/shard_map/write_out/pallas_call | solution.py:473

commit v6 on v5

--- a/solution.py
+++ b/solution.py
@@ -13,6 +13,7 @@
 CHIPS = ROWS * COLUMNS
 CHUNKS = 2
 PARTS = 1
+FIRST = (0,)
 MESH = pl.DeviceIdType.MESH
 F32, BF16 = jnp.float32, jnp.bfloat16
 
@@ -32,9 +33,9 @@
     gain, tok, part, cot_own, cot_part, stage, came, scaled,
     blocks, state_out, state, gathered, scanned, prefix, low,
     weights, attended, stats, grads, late,
-    grad_f32, grad_came,
+    grad_f32, grad_came, early, prefix_part,
     load_sem, core_send, core_recv, go_send, go_recv, back_send, back_recv, stat_send, stat_recv,
-    met, stack_ready,
+    met, stack_ready, twice_send, twice_recv,
 ):
     seq, z = lax.axis_index("seq"), lax.axis_index("head")
     core = lax.rem(seq, 2)
@@ -166,13 +167,28 @@
                 back_send, back_recv.at[s, chunk, colour], {"seq": 2 * target + other, "head": z},
             ).start()
 
+        def twice(target):
+            @pl.when(jnp.logical_and(core == 1, chip != target))
+            def _():
+                remote(
+                    scanned.at[s, chunk, target], prefix_part.at[chunk, my_place],
+                    twice_send, twice_recv.at[chunk, colour], {"seq": 2 * target + 1 + 0 * chip, "head": z},
+                ).start()
+
+            @pl.when(jnp.logical_and(core == 1, chip == target))
+            def _():
+                prefix_part[chunk, my_place] = scanned[s, chunk, target]
+
         if s == 0:
             for target in all_chips:
                 to(target)
         else:
-            to(0 * chip)
+            for target in FIRST:
+                to(target + 0 * chip)
+                twice(target)
             for target in all_chips:
-                pl.when(target != 0)(functools.partial(to, target))
+                ahead = functools.reduce(jnp.logical_or, [target == t for t in FIRST])
+                pl.when(jnp.logical_not(ahead))(functools.partial(to, target))
 
     def scan_back(s, chunk, reverse):
         with jax.named_scope(f"go_wait{s}{chunk}"):
@@ -364,9 +380,19 @@
     def give(n, j):
         return to_core(grad_f32.at[n, other, :, col(j)], grad_came.at[n, :, col(j)], 2, CHUNKS + 2)
 
+    keys_values = grad_came.at[pl.ds(1, 2)]
+    give_early = to_core(early, keys_values, 2, CHUNKS + 2)
+    is_first = functools.reduce(jnp.logical_or, [chip == t for t in FIRST])
     with jax.named_scope("without_suffix"):
         without_suffix(other)
         give_query.start()
+
+        @pl.when(jnp.logical_and(is_first, core == 0))
+        def _():
+            for n in (1, 2):
+                early[n - 1] = grad_f32[n, 1]
+            give_early.start()
+
         without_suffix(core)
         result[0, :, own_cols] = grad_f32[0, core].astype(BF16)
     with jax.named_scope("dq_out"):
@@ -386,8 +412,12 @@
             after = head_of(1, j)
             with_suffix(0, j, (after + late[j]).astype(BF16))
             with_suffix(1, j, after.astype(BF16))
-            for n in (1, 2):
-                give(n, j).start()
+
+            @pl.when(jnp.logical_not(jnp.logical_and(is_first, core == 0)))
+            def _():
+                for n in (1, 2):
+                    give(n, j).start()
+
     with jax.named_scope("own_out"):
         for n in (1, 2):
             result[n, :, own_cols] = grad_f32[n, core].astype(BF16)
@@ -399,11 +429,42 @@
         remote(scanned, scanned, back_send, go_recv.at[0, 0], partner).wait_send()
         all_stats.wait_send()
     with jax.named_scope("final_core"):
-        keys_values = grad_came.at[pl.ds(1, 2)]
         to_core(keys_values, keys_values, 2, CHUNKS + 2).wait_recv()
-        for n in (1, 2):
-            result[n, :, part_cols] = grad_came[n].astype(BF16)
+
+        @pl.when(jnp.logical_not(jnp.logical_and(is_first, core == 1)))
+        def _():
+            for n in (1, 2):
+                result[n, :, part_cols] = grad_came[n].astype(BF16)
+
+        @pl.when(jnp.logical_and(is_first, core == 1))
+        def _():
+            for j in range(heads):
+                chunk, head = divmod(j, 2)
+                for own in range(2):
+
+                    @pl.when((colour == head) == bool(own))
+                    def _():
+                        pieces = prefix_part.at[chunk, pl.ds(head * (CHIPS // 2), CHIPS // 2 - own)]
+                        remote(pieces, pieces, twice_send, twice_recv.at[chunk, head], partner).wait_recv()
+
+            for j in range(heads):
+                at = pl.ds(j % per_chunk * per_head, per_head)
+                suffix = prefix_part[j // per_chunk, at].reshape(HEAD_DIM, HEAD_DIM).astype(BF16)
+                cols = pl.ds(pl.multiple_of(other * mine + j * HEAD_DIM, HEAD_DIM), HEAD_DIM)
+                keys = grad_came[1, :, col(j)] + scale * dot(part[2, :, col(j)], suffix, (1, 1))
+                values = grad_came[2, :, col(j)] + scale * dot(part[1, :, col(j)], suffix, (1, 0))
+                result[1, :, cols] = keys.astype(BF16)
+                result[2, :, cols] = values.astype(BF16)
+
         to_core(grad_came, grad_came, 2, 0).wait_send()
+        for own in range(2):
+            count = CHUNKS * (len(FIRST) - own)
+            if count:
+
+                @pl.when(jnp.logical_and(core == 1, is_first == bool(own)))
+                def _():
+                    pieces = scanned.at[1, 0, pl.ds(0, count)]
+                    remote(pieces, pieces, twice_send, twice_recv.at[0, 0], partner).wait_send()
 
 
 def write_out(result, dq_hbm, dk_hbm, dv_hbm, sems):
@@ -458,11 +519,14 @@
             pltpu.VMEM((heads, HEAD_DIM, HEAD_DIM), F32),
             pltpu.VMEM((3, 2, tokens, mine), F32),
             pltpu.VMEM((3, tokens, mine), F32),
+            pltpu.VMEM((2, tokens, mine), F32),
+            pltpu.VMEM((CHUNKS, CHIPS, piece, HEAD_DIM), F32),
             dma((9,)),
             dma((3,)), dma((CHUNKS + 3,)),
             dma, dma((2, CHUNKS)), dma, dma((2, CHUNKS, 2)),
             dma, dma,
             pltpu.SemaphoreType.REGULAR, pltpu.SemaphoreType.REGULAR,
+            dma, dma((CHUNKS, 2)),
         ],
         compiler_params=pltpu.CompilerParams(
             collective_id=0, has_side_effects=True, vmem_limit_bytes=24 * 1024 * 1024

time: 55.3 us -> 54.7 us (0.989)
  Pallas kernels: 54.6 us -> 53.9 us
    pallas_call x1, Pallas kernels: 53.7 us -> 53 us  [per_device(): pl.pallas_call(functools.partial(kernel, stacks, mine), out_shape=jax.Sha...]
where the time goes in v6:
time: 54.7 us; the launch traced here: 54.5 us
  Pallas kernels  53.9 us (99%)
  between operations  0.64 us (1%)
    pallas_call x1, Pallas kernels, per_device(): pl.pallas_call(functools.partial(kernel, stacks, mine), out_shape=jax.Sha...  53 us

profile of v6, /device:TPU:1, one launch (start us, length us, event | category | flops | bytes accessed | tf_op | source)
XLA Modules:
  0.0 54.5 jit_solution(7052052285483931357)
XLA Ops:
  0.6 53.0 %attention.1.result = bf16[3,128,1024]{2,1,0:T(8,128)(2,1)S(1)} custom-call(bf16[128,1024]{1,0:T(8,128)(2,1)} %q_hbm.1, bf16[128,1024]{1,0:T(8,128)(2,1)} %k_hbm.1, bf16[128,1024]{1,0:T(8,128)(2,1)} %v_hbm.1, bf16[128,1024]{1,0:T(8,128)(2,1)} %cot_hbm.1, f32[8,128]{1,0:T(8,128)} %bitcast.1), custom_call_target="tpu_custom_call" | custom-call | tf_op jit(solution)/shard_map/attention/pallas_call | solution.py:494
  53.6 0.9 %write_out.1 = (bf16[128,1024]{1,0:T(8,128)(2,1)}, bf16[128,1024]{1,0:T(8,128)(2,1)}, bf16[128,1024]{1,0:T(8,128)(2,1)}) custom-call(bf16[3,128,1024]{2,1,0:T(8,128)(2,1)S(1)} %attention.1.result), custom_call_target="tpu_custom_call" | custom-call | tf_op jit(solution)/shard_map/write_out/pallas_call | solution.py:537

commit v7 on v5

--- a/solution.py
+++ b/solution.py
@@ -32,9 +32,9 @@
     gain, tok, part, cot_own, cot_part, stage, came, scaled,
     blocks, state_out, state, gathered, scanned, prefix, low,
     weights, attended, stats, grads, late,
-    grad_f32, grad_came,
+    grad_f32, grad_came, early, prefix_part,
     load_sem, core_send, core_recv, go_send, go_recv, back_send, back_recv, stat_send, stat_recv,
-    met, stack_ready,
+    met, stack_ready, twice_send, twice_recv,
 ):
     seq, z = lax.axis_index("seq"), lax.axis_index("head")
     core = lax.rem(seq, 2)
@@ -166,13 +166,40 @@
                 back_send, back_recv.at[s, chunk, colour], {"seq": 2 * target + other, "head": z},
             ).start()
 
+        def twice(target):
+            remote(
+                scanned.at[s, chunk, target], prefix_part.at[lax.div(chip, 2)],
+                twice_send, twice_recv, {"seq": 2 * target + 1, "head": z},
+            ).start()
+
+        def to_both(target):
+            to(target)
+            twice(target)
+
+        def to_all(one):
+            for target in all_chips[:-1]:
+                pl.when(target != 0)(functools.partial(one, target))
+            pl.when(chip != 0)(functools.partial(to, chip))
+
         if s == 0:
             for target in all_chips:
                 to(target)
+        elif chunk < CHUNKS - 1:
+            to(0 * chip)
+            to_all(to)
         else:
+            owns_last = jnp.logical_and(core == 1, colour == 1)
             to(0 * chip)
-            for target in all_chips:
-                pl.when(target != 0)(functools.partial(to, target))
+
+            @pl.when(jnp.logical_not(owns_last))
+            def _():
+                to_all(to)
+
+            @pl.when(owns_last)
+            def _():
+                pl.when(chip != 0)(functools.partial(twice, 0 * chip))
+                to_all(to_both)
+                prefix_part[lax.div(chip, 2)] = scanned[s, chunk, chip]
 
     def scan_back(s, chunk, reverse):
         with jax.named_scope(f"go_wait{s}{chunk}"):
@@ -364,9 +391,18 @@
     def give(n, j):
         return to_core(grad_f32.at[n, other, :, col(j)], grad_came.at[n, :, col(j)], 2, CHUNKS + 2)
 
+    keys_values = grad_came.at[pl.ds(1, 2)]
+    give_early = to_core(early, grad_came.at[pl.ds(1, 2), :, col(heads - 1)], 2, CHUNKS + 2)
     with jax.named_scope("without_suffix"):
         without_suffix(other)
         give_query.start()
+
+        @pl.when(core == 0)
+        def _():
+            for n in (1, 2):
+                early[n - 1] = grad_f32[n, 1, :, col(heads - 1)]
+            give_early.start()
+
         without_suffix(core)
         result[0, :, own_cols] = grad_f32[0, core].astype(BF16)
     with jax.named_scope("dq_out"):
@@ -386,8 +422,12 @@
             after = head_of(1, j)
             with_suffix(0, j, (after + late[j]).astype(BF16))
             with_suffix(1, j, after.astype(BF16))
-            for n in (1, 2):
-                give(n, j).start()
+
+            @pl.when(core >= (1 if j == heads - 1 else 0))
+            def _():
+                for n in (1, 2):
+                    give(n, j).start()
+
     with jax.named_scope("own_out"):
         for n in (1, 2):
             result[n, :, own_cols] = grad_f32[n, core].astype(BF16)
@@ -399,11 +439,38 @@
         remote(scanned, scanned, back_send, go_recv.at[0, 0], partner).wait_send()
         all_stats.wait_send()
     with jax.named_scope("final_core"):
-        keys_values = grad_came.at[pl.ds(1, 2)]
         to_core(keys_values, keys_values, 2, CHUNKS + 2).wait_recv()
-        for n in (1, 2):
-            result[n, :, part_cols] = grad_came[n].astype(BF16)
+
+        @pl.when(core == 0)
+        def _():
+            for n in (1, 2):
+                result[n, :, part_cols] = grad_came[n].astype(BF16)
+
+        @pl.when(core == 1)
+        def _():
+            rest = (heads - 1) * HEAD_DIM
+            for n in (1, 2):
+                result[n, :, 0:rest] = grad_came[n, :, 0:rest].astype(BF16)
+            for own in range(2):
+
+                @pl.when(colour == own)
+                def _():
+                    pieces = prefix_part.at[pl.ds(0, CHIPS // 2 - own)]
+                    remote(pieces, pieces, twice_send, twice_recv, partner).wait_recv()
+
+            last = col(heads - 1)
+            suffix = prefix_part[...].reshape(HEAD_DIM, HEAD_DIM).astype(BF16)
+            keys = grad_came[1, :, last] + scale * dot(part[2, :, last], suffix, (1, 1))
+            values = grad_came[2, :, last] + scale * dot(part[1, :, last], suffix, (1, 0))
+            result[1, :, last] = keys.astype(BF16)
+            result[2, :, last] = values.astype(BF16)
+
         to_core(grad_came, grad_came, 2, 0).wait_send()
+
+        @pl.when(jnp.logical_and(core == 1, colour == 1))
+        def _():
+            pieces = scanned.at[1, 0, pl.ds(0, CHIPS - 1)]
+            remote(pieces, pieces, twice_send, twice_recv, partner).wait_send()
 
 
 def write_out(result, dq_hbm, dk_hbm, dv_hbm, sems):
@@ -458,11 +525,14 @@
             pltpu.VMEM((heads, HEAD_DIM, HEAD_DIM), F32),
             pltpu.VMEM((3, 2, tokens, mine), F32),
             pltpu.VMEM((3, tokens, mine), F32),
+            pltpu.VMEM((2, tokens, HEAD_DIM), F32),
+            pltpu.VMEM((CHIPS // 2, piece, HEAD_DIM), F32),
             dma((9,)),
             dma((3,)), dma((CHUNKS + 3,)),
             dma, dma((2, CHUNKS)), dma, dma((2, CHUNKS, 2)),
             dma, dma,
             pltpu.SemaphoreType.REGULAR, pltpu.SemaphoreType.REGULAR,
+            dma, dma,
         ],
         compiler_params=pltpu.CompilerParams(
             collective_id=0, has_side_effects=True, vmem_limit_bytes=24 * 1024 * 1024

time: 55.3 us -> 54.8 us (level)
  Pallas kernels: 54.6 us -> 54 us
    pallas_call x1, Pallas kernels: 53.7 us -> 53.1 us  [per_device(): pl.pallas_call(functools.partial(kernel, stacks, mine), out_shape=jax.Sha...]
where the time goes in v7:
time: 54.8 us; the launch traced here: 54.6 us
  Pallas kernels  54 us (99%)
  between operations  0.64 us (1%)
    pallas_call x1, Pallas kernels, per_device(): pl.pallas_call(functools.partial(kernel, stacks, mine), out_shape=jax.Sha...  53.1 us

profile of v7, /device:TPU:1, one launch (start us, length us, event | category | flops | bytes accessed | tf_op | source)
XLA Modules:
  0.0 54.6 jit_solution(2533408424103503434)
XLA Ops:
  0.6 53.1 %attention.1.result = bf16[3,128,1024]{2,1,0:T(8,128)(2,1)S(1)} custom-call(bf16[128,1024]{1,0:T(8,128)(2,1)} %q_hbm.1, bf16[128,1024]{1,0:T(8,128)(2,1)} %k_hbm.1, bf16[128,1024]{1,0:T(8,128)(2,1)} %v_hbm.1, bf16[128,1024]{1,0:T(8,128)(2,1)} %cot_hbm.1, f32[8,128]{1,0:T(8,128)} %bitcast.1), custom_call_target="tpu_custom_call" | custom-call | tf_op jit(solution)/shard_map/attention/pallas_call | solution.py:500
  53.7 0.9 %write_out.1 = (bf16[128,1024]{1,0:T(8,128)(2,1)}, bf16[128,1024]{1,0:T(8,128)(2,1)}, bf16[128,1024]{1,0:T(8,128)(2,1)}) custom-call(bf16[3,128,1024]{2,1,0:T(8,128)(2,1)S(1)} %attention.1.result), custom_call_target="tpu_custom_call" | custom-call | tf_op jit(solution)/shard_map/write_out/pallas_call | solution.py:543

commit v8 on v6

--- a/solution.py
+++ b/solution.py
@@ -447,7 +447,6 @@
                         pieces = prefix_part.at[chunk, pl.ds(head * (CHIPS // 2), CHIPS // 2 - own)]
                         remote(pieces, pieces, twice_send, twice_recv.at[chunk, head], partner).wait_recv()
 
-            for j in range(heads):
                 at = pl.ds(j % per_chunk * per_head, per_head)
                 suffix = prefix_part[j // per_chunk, at].reshape(HEAD_DIM, HEAD_DIM).astype(BF16)
                 cols = pl.ds(pl.multiple_of(other * mine + j * HEAD_DIM, HEAD_DIM), HEAD_DIM)

time: 54.7 us -> 54.7 us (level)
  no operation moved by 1% of the time
where the time goes in v8:
time: 54.7 us; the launch traced here: 54.5 us
  Pallas kernels  53.9 us (99%)
  between operations  0.64 us (1%)
    pallas_call x1, Pallas kernels, per_device(): pl.pallas_call(functools.partial(kernel, stacks, mine), out_shape=jax.Sha...  53 us

profile of v8, /device:TPU:1, one launch (start us, length us, event | category | flops | bytes accessed | tf_op | source)
XLA Modules:
  0.0 54.5 jit_solution(6401797326447591984)
XLA Ops:
  0.6 53.0 %attention.1.result = bf16[3,128,1024]{2,1,0:T(8,128)(2,1)S(1)} custom-call(bf16[128,1024]{1,0:T(8,128)(2,1)} %q_hbm.1, bf16[128,1024]{1,0:T(8,128)(2,1)} %k_hbm.1, bf16[128,1024]{1,0:T(8,128)(2,1)} %v_hbm.1, bf16[128,1024]{1,0:T(8,128)(2,1)} %cot_hbm.1, f32[8,128]{1,0:T(8,128)} %bitcast.1), custom_call_target="tpu_custom_call" | custom-call | tf_op jit(solution)/shard_map/attention/pallas_call | solution.py:493
  53.6 0.9 %write_out.1 = (bf16[128,1024]{1,0:T(8,128)(2,1)}, bf16[128,1024]{1,0:T(8,128)(2,1)}, bf16[128,1024]{1,0:T(8,128)(2,1)}) custom-call(bf16[3,128,1024]{2,1,0:T(8,128)(2,1)S(1)} %attention.1.result), custom_call_target="tpu_custom_call" | custom-call | tf_op jit(solution)/shard_map/write_out/pallas_call | solution.py:536
